TPU v7x, 1024 devices: a whole 4x4x32 slice. The times are simulated.
1024 devices in a mesh: agg: 8 (over y, core), gx: 32 (over z_lo, x), gy: 4 (over z_hi).
Axes of the slice: x: 4, y: 4, z: 32 (z_hi: 4, z_lo: 8; z = z_hi * 8 + z_lo), core: 2. Of those that a mesh axis runs over, the one named last changes fastest.
Arguments:
- velocity_prev: float32 [3, 256, 64, 1024], P(None, 'gx', 'gy', 'agg'), may hold values from -6 to 6
- forcing: float32 [3, 256, 64, 1024], P(None, 'gx', 'gy', 'agg'), may hold values from -6 to 6
- reaction: float32 [256, 64, 1024], P('gx', 'gy', 'agg'), may hold values from 0.1 to 4
Outputs:
- velocity: float32 [3, 256, 64, 1024], P(None, 'gx', 'gy', 'agg')
- compressed: float32 [3, 64, 1024, 128], P(None, 'gy', ('agg', 'gx'))
All inputs are finite; a program needn't handle non-finite values.
Results may differ from a plain program's by a relative error of at most 0.00002.
Values sent between devices are 32-bit elements; how exact they have to be, the bound alone decides.
A program may use at most 64 MiB of HBM per device.

v0:
```python
import jax
import jax.numpy as jnp
from jax import lax
from jax.sharding import PartitionSpec as P

SWEEPS = 2
COARSE_SWEEPS = 4
LX = 5


damping = 0.8
root_half = 0.7071067811865476


def extended_2(array, sides, width):
    edges = {}
    for axis, dim in sides:
        devices, length = (lax.axis_size(axis), array.shape[dim])
        up = [(i, (i + 1) % devices) for i in range(devices - 1)]
        last = lax.slice_in_dim(array, length - width, length, axis=dim)
        first = lax.slice_in_dim(array, 0, width, axis=dim)
        edges[dim] = (
            lax.ppermute(last, axis, up),
            lax.ppermute(first, axis, [(b, a) for a, b in up]),
        )
    done = []
    for _, dim in sides:
        low, high = edges[dim]
        around = [(width, width) if d in done else (0, 0) for d in range(array.ndim)]
        array = jnp.concatenate([jnp.pad(low, around), array, jnp.pad(high, around)], axis=dim)
        done.append(dim)
    return array


def padded_2(block, sides, width):
    for axis, dim in sides:
        count = lax.axis_size(axis)
        forward = [(i, i + 1) for i in range(count - 1)]
        backward = [(target, source) for source, target in forward]
        low = lax.ppermute(
            lax.slice_in_dim(block, block.shape[dim] - width, None, axis=dim), axis, forward
        )
        high = lax.ppermute(lax.slice_in_dim(block, 0, width, axis=dim), axis, backward)
        block = jnp.concatenate([low, block, high], axis=dim)
    return block


def neighbours(padded):
    summed = padded[:, 2:, 1:-1, 1:-1] + padded[:, :-2, 1:-1, 1:-1]
    summed = summed + padded[:, 1:-1, 2:, 1:-1] + padded[:, 1:-1, :-2, 1:-1]
    summed = summed + padded[:, 1:-1, 1:-1, 2:] + padded[:, 1:-1, 1:-1, :-2]
    return summed


def trim_cells(values, depth):
    return values[:, depth:-depth, depth:-depth, depth:-depth]


def along_axis(count, depth, position, devices):
    spots = position * count + jnp.arange(count + 2 * depth, dtype=jnp.int32) - depth
    inside = (spots >= 0) & (spots < count * devices)
    return inside.astype(jnp.float32)


def valid_mask(cells_x, cells_y, cells_z, depth):
    mask_x = along_axis(cells_x, depth, lax.axis_index("gx"), lax.axis_size("gx"))
    mask_y = along_axis(cells_y, depth, lax.axis_index("gy"), lax.axis_size("gy"))
    mask_z = along_axis(cells_z, depth, lax.axis_index("agg"), lax.axis_size("agg"))
    return (mask_x[:, None, None] * mask_y[None, :, None] * mask_z[None, None, :])[None]


def last_residual(current, forcing, diagonal):
    padded = extended_2(current, (("agg", 3), ("gx", 1), ("gy", 2)), 1)
    return forcing - (diagonal * current - neighbours(padded))


def each_residual(current, forcing, diagonal):
    padded = extended_2(current, (("agg", 3), ("gx", 1), ("gy", 2)), 1)
    return forcing - (diagonal * current - neighbours(padded))


def block_mean(field):
    components, size_x, size_y, size_z = field.shape
    return field.reshape(components, size_x // 2, 2, size_y // 2, 2, size_z // 2, 2).mean(
        axis=(2, 4, 6)
    )


def prolong(coarse):
    components, size_x, size_y, size_z = coarse.shape
    expanded = jnp.broadcast_to(
        coarse[:, :, None, :, None, :, None], (components, size_x, 2, size_y, 2, size_z, 2)
    )
    return expanded.reshape(components, 2 * size_x, 2 * size_y, 2 * size_z)


def halve_last(values):
    paired = values.reshape(values.shape[:-1] + (values.shape[-1] // 2, 2))
    even_cells = paired[..., 0]
    odd_cells = paired[..., 1]
    return ((even_cells + odd_cells) * root_half, (even_cells - odd_cells) * root_half)


def x_levels(approx):
    details = []
    for level_index in range(LX - 1):
        approx, detail = halve_last(approx)
        details.append(detail)
    return jnp.concatenate([approx] + details[::-1], axis=-1)


def pair_pass(values, which_dim):
    layout = values.shape
    paired = values.reshape(
        layout[:which_dim] + (layout[which_dim] // 2, 2) + layout[which_dim + 1 :]
    )
    even_cells = lax.index_in_dim(paired, 0, which_dim + 1, keepdims=False)
    odd_cells = lax.index_in_dim(paired, 1, which_dim + 1, keepdims=False)
    stacked = jnp.stack(
        [(even_cells + odd_cells) * root_half, (even_cells - odd_cells) * root_half],
        axis=which_dim + 1,
    )
    return stacked.reshape(layout)


def finish_lines(x_lines):
    coeffs = x_levels(x_lines)
    return pair_pass(pair_pass(coeffs, 1), 2)


def on_device(velocity_prev, forcing, reaction):
    components, cells_x, cells_y, cells_z = velocity_prev.shape
    diagonal = (6.0 + reaction)[None]
    current = velocity_prev
    for sweep_index in range(SWEEPS):
        current = current + damping * each_residual(current, forcing, diagonal) / diagonal
    fine_res = each_residual(current, forcing, diagonal)
    coarse_rhs = block_mean(fine_res)
    coarse_diag = (6.0 + 4.0 * block_mean(reaction[None])) * 0.25
    reach = COARSE_SWEEPS - 1
    stacked = jnp.concatenate([coarse_rhs, coarse_diag], axis=0)
    extended = padded_2(stacked, (("agg", 3), ("gx", 1), ("gy", 2)), reach)
    inside = valid_mask(cells_x // 2, cells_y // 2, cells_z // 2, reach)
    rhs_ext = extended[:3]
    diag_ext = extended[3:4] * inside + (1.0 - inside)
    correction = inside * damping * rhs_ext / diag_ext
    for sweep_index in range(reach):
        shrink = sweep_index + 1
        center = trim_cells(correction, 1)
        rhs_in = trim_cells(rhs_ext, shrink)
        diag_in = trim_cells(diag_ext, shrink)
        update = damping * (rhs_in - (diag_in * center - 0.25 * neighbours(correction))) / diag_in
        correction = center + trim_cells(inside, shrink) * update
    current = current + prolong(correction)
    velocity = current + damping * last_residual(current, forcing, diagonal) / diagonal
    x_lines = jnp.transpose(
        lax.all_to_all(velocity_prev, "gx", split_axis=3, concat_axis=1, tiled=True), (0, 2, 3, 1)
    )
    compressed = finish_lines(halve_last(x_lines)[0])
    return (velocity, compressed)


def solution(mesh):
    placed = (P(None, "gx", "gy", "agg"), P(None, "gx", "gy", "agg"), P("gx", "gy", "agg"))
    return jax.shard_map(
        on_device,
        mesh=mesh,
        in_specs=placed,
        out_specs=(P(None, "gx", "gy", "agg"), P(None, "gy", ("agg", "gx"), None)),
        check_vma=False,
    )
```

profile of v0, /device:TPU:232, one launch (start us, length us, event | category | flops | bytes accessed | tf_op | source)
XLA Modules:
  0.0 266.1 jit_solution(13376346738120731162)
XLA Ops:
  8.3 15.7 %collective-permute-start.5 = (f32[3,8,1,128]{3,2,1,0:T(1,128)S(1)}, f32[3,8,1,128]{3,2,1,0:T(1,128)S(1)}, u32[]{:S(2)}, u32[]{:S(2)}) collective-permute-start(f32[3,8,1,128]{3,2,1,0:T(1,128)S(1)} %get-tuple-element.41), channel_id=1, source_target_pairs={{0,1},{1,2},{2,3},{4,5},{5,6},{6,7},{8,9},{9,10},{10,11},{12,13},{... | collective-permute-start | bytes 36872 | tf_op jit(solution)/shard_map/ppermute | solution.py:23
  24.8 4.2 %collective-permute-start.2 = (f32[3,1,16,128]{3,2,1,0:T(8,128)S(1)}, f32[3,1,16,128]{3,2,1,0:T(8,128)S(1)}, u32[]{:S(2)}, u32[]{:S(2)}) collective-permute-start(f32[3,1,16,128]{3,2,1,0:T(8,128)S(1)} %get-tuple-element.43), channel_id=1, source_target_pairs={{4,0},{8,4},{12,8},{16,12},{20,16},{24,20},{28,24},{32,28},{36,32}... | collective-permute-start | bytes 73736 | tf_op jit(solution)/shard_map/ppermute | solution.py:24
  33.8 12.8 %all-to-all-start = ((f32[32,1,1536]{2,1,0:T(1,128)}), f32[32,1,1536]{2,1,0:T(1,128)S(1)}, u32[]{:S(2)}, u32[]{:S(2)}) async-start(f32[32,1,1536]{2,1,0:T(1,128)} %reshape.168), calls=%async_computation | async-start | bytes 393216 | tf_op jit(solution)/shard_map/all_to_all | solution.py:157
  46.6 5.6 %reshape_broadcast_in_dim.3 = f32[4,2,8,2,64,2]{5,4,3,2,1,0:T(8,128)} reshape(f32[8,16,128]{2,1,0:T(8,128)S(1)} %copy-done.2) | data formatting | bytes 131072 | tf_op jit(solution)/shard_map/reshape;broadcast_in_dim | solution.py:84
  56.3 12.9 %collective-permute-done.4 = f32[3,8,1,128]{3,2,1,0:T(1,128)S(1)} collective-permute-done((f32[3,8,1,128]{3,2,1,0:T(1,128)S(1)}, f32[3,8,1,128]{3,2,1,0:T(1,128)S(1)}, u32[]{:S(2)}, u32[]{:S(2)}) %collective-permute-start.4) | collective-permute-done | bytes 12320 | tf_op jit(solution)/shard_map/ppermute | solution.py:24
  69.8 4.6 %collective-permute-start.8 = (f32[3,1,16,128]{3,2,1,0:T(8,128)S(1)}, f32[3,1,16,128]{3,2,1,0:T(8,128)S(1)}, u32[]{:S(2)}, u32[]{:S(2)}) collective-permute-start(f32[3,1,16,128]{3,2,1,0:T(8,128)S(1)} %get-tuple-element.37), channel_id=1, source_target_pairs={{4,0},{8,4},{12,8},{16,12},{20,16},{24,20},{28,24},{32,28},{36,32}... | collective-permute-start | bytes 73736 | tf_op jit(solution)/shard_map/ppermute | solution.py:24
  80.0 9.0 %collective-permute-start.11 = (f32[3,8,1,128]{3,2,1,0:T(1,128)S(1)}, f32[3,8,1,128]{3,2,1,0:T(1,128)S(1)}, u32[]{:S(2)}, u32[]{:S(2)}) collective-permute-start(f32[3,8,1,128]{3,2,1,0:T(1,128)S(1)} %get-tuple-element.35), channel_id=1, source_target_pairs={{0,1},{1,2},{2,3},{4,5},{5,6},{6,7},{8,9},{9,10},{10,11},{12,13},{... | collective-permute-start | bytes 36872 | tf_op jit(solution)/shard_map/ppermute | solution.py:23
  92.3 4.5 %collective-permute-done.9 = f32[3,1,16,128]{3,2,1,0:T(8,128)S(1)} collective-permute-done((f32[3,1,16,128]{3,2,1,0:T(8,128)S(1)}, f32[3,1,16,128]{3,2,1,0:T(8,128)S(1)}, u32[]{:S(2)}, u32[]{:S(2)}) %collective-permute-start.9) | collective-permute-done | bytes 24608 | tf_op jit(solution)/shard_map/ppermute | solution.py:23
  96.9 8.3 %collective-permute-done.10 = f32[3,8,1,128]{3,2,1,0:T(1,128)S(1)} collective-permute-done((f32[3,8,1,128]{3,2,1,0:T(1,128)S(1)}, f32[3,8,1,128]{3,2,1,0:T(1,128)S(1)}, u32[]{:S(2)}, u32[]{:S(2)}) %collective-permute-start.10) | collective-permute-done | bytes 12320 | tf_op jit(solution)/shard_map/ppermute | solution.py:24
  105.8 6.0 %collective-permute-start.14 = (f32[3,1,16,128]{3,2,1,0:T(8,128)S(1)}, f32[3,1,16,128]{3,2,1,0:T(8,128)S(1)}, u32[]{:S(2)}, u32[]{:S(2)}) collective-permute-start(f32[3,1,16,128]{3,2,1,0:T(8,128)S(1)} %get-tuple-element.31), channel_id=1, source_target_pairs={{4,0},{8,4},{12,8},{16,12},{20,16},{24,20},{28,24},{32,28},{36,32}... | collective-permute-start | bytes 73736 | tf_op jit(solution)/shard_map/ppermute | solution.py:24
  117.5 6.1 %collective-permute-start.17 = (f32[3,8,1,128]{3,2,1,0:T(1,128)S(1)}, f32[3,8,1,128]{3,2,1,0:T(1,128)S(1)}, u32[]{:S(2)}, u32[]{:S(2)}) collective-permute-start(f32[3,8,1,128]{3,2,1,0:T(1,128)S(1)} %get-tuple-element.29), channel_id=1, source_target_pairs={{0,1},{1,2},{2,3},{4,5},{5,6},{6,7},{8,9},{9,10},{10,11},{12,13},{... | collective-permute-start | bytes 36872 | tf_op jit(solution)/shard_map/ppermute | solution.py:23
  126.9 4.5 %collective-permute-done.15 = f32[3,1,16,128]{3,2,1,0:T(8,128)S(1)} collective-permute-done((f32[3,1,16,128]{3,2,1,0:T(8,128)S(1)}, f32[3,1,16,128]{3,2,1,0:T(8,128)S(1)}, u32[]{:S(2)}, u32[]{:S(2)}) %collective-permute-start.15) | collective-permute-done | bytes 24608 | tf_op jit(solution)/shard_map/ppermute | solution.py:23
  131.5 8.3 %collective-permute-done.16 = f32[3,8,1,128]{3,2,1,0:T(1,128)S(1)} collective-permute-done((f32[3,8,1,128]{3,2,1,0:T(1,128)S(1)}, f32[3,8,1,128]{3,2,1,0:T(1,128)S(1)}, u32[]{:S(2)}, u32[]{:S(2)}) %collective-permute-start.16) | collective-permute-done | bytes 12320 | tf_op jit(solution)/shard_map/ppermute | solution.py:24
  140.3 14.0 %reshape.164 = f32[3,4,2,8,2,64,2]{6,5,4,3,2,1,0:T(8,128)} reshape(f32[3,8,16,128]{3,2,1,0:T(8,128)S(1)} %fusion.22) | data formatting | bytes 393216 | tf_op jit(solution)/shard_map/reshape | solution.py:84
  154.3 5.5 %reduce_sum.18 = f32[3,4,8,64]{3,2,1,0:T(8,128)S(1)} reduce(f32[3,4,2,8,2,64,2]{6,5,4,3,2,1,0:T(8,128)} %reshape.164, f32[]{:T(128)} %constant.21.clone.1), dimensions={2,4,6}, to_apply=%region_0.1 | reduce | flops 43008 | bytes 221188 | tf_op jit(solution)/shard_map/reduce_sum | solution.py:84
  167.5 6.0 %collective-permute-start.21 = (f32[4,3,8,70]{3,2,1,0:T(8,128)S(1)}, f32[4,3,8,70]{3,2,1,0:T(8,128)S(1)}, u32[]{:S(2)}, u32[]{:S(2)}) collective-permute-start(f32[4,3,8,70]{3,2,1,0:T(8,128)S(1)} %get-tuple-element.57), channel_id=1, source_target_pairs={{4,0},{8,4},{12,8},{16,12},{20,16},{24,20},{28,24},{32,28},{36,32}... | collective-permute-start | bytes 80648 | tf_op jit(solution)/shard_map/ppermute | solution.py:43
  175.5 6.1 %collective-permute-done.20 = f32[4,3,8,70]{3,2,1,0:T(8,128)S(1)} collective-permute-done((f32[4,3,8,70]{3,2,1,0:T(8,128)S(1)}, f32[4,3,8,70]{3,2,1,0:T(8,128)S(1)}, u32[]{:S(2)}, u32[]{:S(2)}) %collective-permute-start.20) | collective-permute-done | bytes 26912 | tf_op jit(solution)/shard_map/ppermute | solution.py:40
  183.1 13.3 %collective-permute-start.22 = (f32[4,10,3,70]{3,2,1,0:T(4,128)S(1)}, f32[4,10,3,70]{3,2,1,0:T(4,128)S(1)}, u32[]{:S(2)}, u32[]{:S(2)}) collective-permute-start(f32[4,10,3,70]{3,2,1,0:T(4,128)S(1)} %get-tuple-element.46), channel_id=1, source_target_pairs={{0,1},{1,2},{2,3},{4,5},{5,6},{6,7},{8,9},{9,10},{10,11},{12,13},{... | collective-permute-start | bytes 100808 | tf_op jit(solution)/shard_map/ppermute | solution.py:40
  199.0 7.2 %collective-permute-done.22 = f32[4,10,3,70]{3,2,1,0:T(4,128)S(1)} collective-permute-done((f32[4,10,3,70]{3,2,1,0:T(4,128)S(1)}, f32[4,10,3,70]{3,2,1,0:T(4,128)S(1)}, u32[]{:S(2)}, u32[]{:S(2)}) %collective-permute-start.22) | collective-permute-done | bytes 33632 | tf_op jit(solution)/shard_map/ppermute | solution.py:40
  207.8 5.2 %broadcast_in_dim.2 = f32[3,4,2,8,2,64,2]{6,5,4,3,2,1,0:T(8,128)} broadcast(f32[3,4,8,64]{3,2,1,0:T(8,128)S(1)} %fusion.67), dimensions={0,1,3,5} | broadcast | bytes 221184 | tf_op jit(solution)/shard_map/broadcast_in_dim | solution.py:91
  213.0 9.8 %reshape.165 = f32[3,8,16,128]{3,2,1,0:T(8,128)S(1)} reshape(f32[3,4,2,8,2,64,2]{6,5,4,3,2,1,0:T(8,128)} %broadcast_in_dim.2) | data formatting | bytes 393216 | tf_op jit(solution)/shard_map/reshape | solution.py:94
  222.9 13.2 %collective-permute-start.29 = (f32[3,8,1,128]{3,2,1,0:T(1,128)S(1)}, f32[3,8,1,128]{3,2,1,0:T(1,128)S(1)}, u32[]{:S(2)}, u32[]{:S(2)}) collective-permute-start(f32[3,8,1,128]{3,2,1,0:T(1,128)S(1)} %get-tuple-element.23), channel_id=1, source_target_pairs={{0,1},{1,2},{2,3},{4,5},{5,6},{6,7},{8,9},{9,10},{10,11},{12,13},{... | collective-permute-start | bytes 36872 | tf_op jit(solution)/shard_map/ppermute | solution.py:23
  238.0 3.9 %collective-permute-start.27 = (f32[3,1,16,128]{3,2,1,0:T(8,128)S(1)}, f32[3,1,16,128]{3,2,1,0:T(8,128)S(1)}, u32[]{:S(2)}, u32[]{:S(2)}) collective-permute-start(f32[3,1,16,128]{3,2,1,0:T(8,128)S(1)} %get-tuple-element.24), channel_id=1, source_target_pairs={{0,4},{4,8},{8,12},{12,16},{16,20},{20,24},{24,28},{28,32},{32,36}... | collective-permute-start | bytes 73736 | tf_op jit(solution)/shard_map/ppermute | solution.py:23
  252.1 4.1 %collective-permute-done.28 = f32[3,8,1,128]{3,2,1,0:T(1,128)S(1)} collective-permute-done((f32[3,8,1,128]{3,2,1,0:T(1,128)S(1)}, f32[3,8,1,128]{3,2,1,0:T(1,128)S(1)}, u32[]{:S(2)}, u32[]{:S(2)}) %collective-permute-start.28) | collective-permute-done | bytes 12320 | tf_op jit(solution)/shard_map/ppermute | solution.py:24
  (130 shorter events, 73.7 us)
Async XLA Ops:
  1.8 54.5 %collective-permute-start = (f32[3,8,16,1]{3,2,1,0:T(8,128)S(1)}, f32[3,8,16,1]{3,2,1,0:T(8,128)S(1)}, u32[]{:S(2)}, u32[]{:S(2)}) collective-permute-start(f32[3,8,16,1]{3,2,1,0:T(8,128)S(1)} %get-tuple-element.45), channel_id=1, source_target_pairs={{0,128},{128,256},{256,384},{384,512},{512,640},{640,768},{768,896... | collective-permute-start | bytes 4616 | tf_op jit(solution)/shard_map/ppermute | solution.py:23
  3.7 52.6 %collective-permute-start.1 = (f32[3,8,16,1]{3,2,1,0:T(8,128)S(1)}, f32[3,8,16,1]{3,2,1,0:T(8,128)S(1)}, u32[]{:S(2)}, u32[]{:S(2)}) collective-permute-start(f32[3,8,16,1]{3,2,1,0:T(8,128)S(1)} %get-tuple-element.44), channel_id=1, source_target_pairs={{128,0},{256,128},{384,256},{512,384},{640,512},{768,640},{896,768... | collective-permute-start | bytes 4616 | tf_op jit(solution)/shard_map/ppermute | solution.py:24
  8.3 48.0 %collective-permute-start.5 = (f32[3,8,1,128]{3,2,1,0:T(1,128)S(1)}, f32[3,8,1,128]{3,2,1,0:T(1,128)S(1)}, u32[]{:S(2)}, u32[]{:S(2)}) collective-permute-start(f32[3,8,1,128]{3,2,1,0:T(1,128)S(1)} %get-tuple-element.41), channel_id=1, source_target_pairs={{0,1},{1,2},{2,3},{4,5},{5,6},{6,7},{8,9},{9,10},{10,11},{12,13},{... | collective-permute-start | bytes 36872 | tf_op jit(solution)/shard_map/ppermute | solution.py:23
  24.8 30.0 %collective-permute-start.2 = (f32[3,1,16,128]{3,2,1,0:T(8,128)S(1)}, f32[3,1,16,128]{3,2,1,0:T(8,128)S(1)}, u32[]{:S(2)}, u32[]{:S(2)}) collective-permute-start(f32[3,1,16,128]{3,2,1,0:T(8,128)S(1)} %get-tuple-element.43), channel_id=1, source_target_pairs={{4,0},{8,4},{12,8},{16,12},{20,16},{24,20},{28,24},{32,28},{36,32}... | collective-permute-start | bytes 73736 | tf_op jit(solution)/shard_map/ppermute | solution.py:24
  29.0 27.2 %collective-permute-start.3 = (f32[3,1,16,128]{3,2,1,0:T(8,128)S(1)}, f32[3,1,16,128]{3,2,1,0:T(8,128)S(1)}, u32[]{:S(2)}, u32[]{:S(2)}) collective-permute-start(f32[3,1,16,128]{3,2,1,0:T(8,128)S(1)} %get-tuple-element.42), channel_id=1, source_target_pairs={{0,4},{4,8},{8,12},{12,16},{16,20},{20,24},{24,28},{28,32},{32,36}... | collective-permute-start | bytes 73736 | tf_op jit(solution)/shard_map/ppermute | solution.py:23
  33.8 223.5 %all-to-all-start = ((f32[32,1,1536]{2,1,0:T(1,128)}), f32[32,1,1536]{2,1,0:T(1,128)S(1)}, u32[]{:S(2)}, u32[]{:S(2)}) async-start(f32[32,1,1536]{2,1,0:T(1,128)} %reshape.168), calls=%async_computation | async-start | bytes 393216 | tf_op jit(solution)/shard_map/all_to_all | solution.py:157
  54.8 14.4 %collective-permute-start.4 = (f32[3,8,1,128]{3,2,1,0:T(1,128)S(1)}, f32[3,8,1,128]{3,2,1,0:T(1,128)S(1)}, u32[]{:S(2)}, u32[]{:S(2)}) collective-permute-start(f32[3,8,1,128]{3,2,1,0:T(1,128)S(1)} %get-tuple-element.40), channel_id=1, source_target_pairs={{1,0},{2,1},{3,2},{5,4},{6,5},{7,6},{9,8},{10,9},{11,10},{13,12},{... | collective-permute-start | bytes 36872 | tf_op jit(solution)/shard_map/ppermute | solution.py:24
  69.8 21.1 %collective-permute-start.8 = (f32[3,1,16,128]{3,2,1,0:T(8,128)S(1)}, f32[3,1,16,128]{3,2,1,0:T(8,128)S(1)}, u32[]{:S(2)}, u32[]{:S(2)}) collective-permute-start(f32[3,1,16,128]{3,2,1,0:T(8,128)S(1)} %get-tuple-element.37), channel_id=1, source_target_pairs={{4,0},{8,4},{12,8},{16,12},{20,16},{24,20},{28,24},{32,28},{36,32}... | collective-permute-start | bytes 73736 | tf_op jit(solution)/shard_map/ppermute | solution.py:24
  74.4 22.5 %collective-permute-start.6 = (f32[3,8,16,1]{3,2,1,0:T(8,128)S(1)}, f32[3,8,16,1]{3,2,1,0:T(8,128)S(1)}, u32[]{:S(2)}, u32[]{:S(2)}) collective-permute-start(f32[3,8,16,1]{3,2,1,0:T(8,128)S(1)} %get-tuple-element.39), channel_id=1, source_target_pairs={{0,128},{128,256},{256,384},{384,512},{512,640},{640,768},{768,896... | collective-permute-start | bytes 4616 | tf_op jit(solution)/shard_map/ppermute | solution.py:23
  76.3 20.6 %collective-permute-start.7 = (f32[3,8,16,1]{3,2,1,0:T(8,128)S(1)}, f32[3,8,16,1]{3,2,1,0:T(8,128)S(1)}, u32[]{:S(2)}, u32[]{:S(2)}) collective-permute-start(f32[3,8,16,1]{3,2,1,0:T(8,128)S(1)} %get-tuple-element.38), channel_id=1, source_target_pairs={{128,0},{256,128},{384,256},{512,384},{640,512},{768,640},{896,768... | collective-permute-start | bytes 4616 | tf_op jit(solution)/shard_map/ppermute | solution.py:24
  80.0 16.9 %collective-permute-start.11 = (f32[3,8,1,128]{3,2,1,0:T(1,128)S(1)}, f32[3,8,1,128]{3,2,1,0:T(1,128)S(1)}, u32[]{:S(2)}, u32[]{:S(2)}) collective-permute-start(f32[3,8,1,128]{3,2,1,0:T(1,128)S(1)} %get-tuple-element.35), channel_id=1, source_target_pairs={{0,1},{1,2},{2,3},{4,5},{5,6},{6,7},{8,9},{9,10},{10,11},{12,13},{... | collective-permute-start | bytes 36872 | tf_op jit(solution)/shard_map/ppermute | solution.py:23
  91.0 14.3 %collective-permute-start.10 = (f32[3,8,1,128]{3,2,1,0:T(1,128)S(1)}, f32[3,8,1,128]{3,2,1,0:T(1,128)S(1)}, u32[]{:S(2)}, u32[]{:S(2)}) collective-permute-start(f32[3,8,1,128]{3,2,1,0:T(1,128)S(1)} %get-tuple-element.34), channel_id=1, source_target_pairs={{1,0},{2,1},{3,2},{5,4},{6,5},{7,6},{9,8},{10,9},{11,10},{13,12},{... | collective-permute-start | bytes 36872 | tf_op jit(solution)/shard_map/ppermute | solution.py:24
  105.8 19.7 %collective-permute-start.14 = (f32[3,1,16,128]{3,2,1,0:T(8,128)S(1)}, f32[3,1,16,128]{3,2,1,0:T(8,128)S(1)}, u32[]{:S(2)}, u32[]{:S(2)}) collective-permute-start(f32[3,1,16,128]{3,2,1,0:T(8,128)S(1)} %get-tuple-element.31), channel_id=1, source_target_pairs={{4,0},{8,4},{12,8},{16,12},{20,16},{24,20},{28,24},{32,28},{36,32}... | collective-permute-start | bytes 73736 | tf_op jit(solution)/shard_map/ppermute | solution.py:24
  111.9 19.6 %collective-permute-start.12 = (f32[3,8,16,1]{3,2,1,0:T(8,128)S(1)}, f32[3,8,16,1]{3,2,1,0:T(8,128)S(1)}, u32[]{:S(2)}, u32[]{:S(2)}) collective-permute-start(f32[3,8,16,1]{3,2,1,0:T(8,128)S(1)} %get-tuple-element.33), channel_id=1, source_target_pairs={{0,128},{128,256},{256,384},{384,512},{512,640},{640,768},{768,896... | collective-permute-start | bytes 4616 | tf_op jit(solution)/shard_map/ppermute | solution.py:23
  113.8 17.7 %collective-permute-start.13 = (f32[3,8,16,1]{3,2,1,0:T(8,128)S(1)}, f32[3,8,16,1]{3,2,1,0:T(8,128)S(1)}, u32[]{:S(2)}, u32[]{:S(2)}) collective-permute-start(f32[3,8,16,1]{3,2,1,0:T(8,128)S(1)} %get-tuple-element.32), channel_id=1, source_target_pairs={{128,0},{256,128},{384,256},{512,384},{640,512},{768,640},{896,768... | collective-permute-start | bytes 4616 | tf_op jit(solution)/shard_map/ppermute | solution.py:24
  117.5 14.0 %collective-permute-start.17 = (f32[3,8,1,128]{3,2,1,0:T(1,128)S(1)}, f32[3,8,1,128]{3,2,1,0:T(1,128)S(1)}, u32[]{:S(2)}, u32[]{:S(2)}) collective-permute-start(f32[3,8,1,128]{3,2,1,0:T(1,128)S(1)} %get-tuple-element.29), channel_id=1, source_target_pairs={{0,1},{1,2},{2,3},{4,5},{5,6},{6,7},{8,9},{9,10},{10,11},{12,13},{... | collective-permute-start | bytes 36872 | tf_op jit(solution)/shard_map/ppermute | solution.py:23
  125.5 14.3 %collective-permute-start.16 = (f32[3,8,1,128]{3,2,1,0:T(1,128)S(1)}, f32[3,8,1,128]{3,2,1,0:T(1,128)S(1)}, u32[]{:S(2)}, u32[]{:S(2)}) collective-permute-start(f32[3,8,1,128]{3,2,1,0:T(1,128)S(1)} %get-tuple-element.28), channel_id=1, source_target_pairs={{1,0},{2,1},{3,2},{5,4},{6,5},{7,6},{9,8},{10,9},{11,10},{13,12},{... | collective-permute-start | bytes 36872 | tf_op jit(solution)/shard_map/ppermute | solution.py:24
  173.5 8.1 %collective-permute-start.20 = (f32[4,3,8,70]{3,2,1,0:T(8,128)S(1)}, f32[4,3,8,70]{3,2,1,0:T(8,128)S(1)}, u32[]{:S(2)}, u32[]{:S(2)}) collective-permute-start(f32[4,3,8,70]{3,2,1,0:T(8,128)S(1)} %get-tuple-element.56), channel_id=1, source_target_pairs={{0,4},{4,8},{8,12},{12,16},{16,20},{20,24},{24,28},{28,32},{32,36}... | collective-permute-start | bytes 80648 | tf_op jit(solution)/shard_map/ppermute | solution.py:40
  181.8 17.3 %collective-permute-start.23 = (f32[4,10,3,70]{3,2,1,0:T(4,128)S(1)}, f32[4,10,3,70]{3,2,1,0:T(4,128)S(1)}, u32[]{:S(2)}, u32[]{:S(2)}) collective-permute-start(f32[4,10,3,70]{3,2,1,0:T(4,128)S(1)} %get-tuple-element.47), channel_id=1, source_target_pairs={{1,0},{2,1},{3,2},{5,4},{6,5},{7,6},{9,8},{10,9},{11,10},{13,12},{... | collective-permute-start | bytes 100808 | tf_op jit(solution)/shard_map/ppermute | solution.py:43
  183.1 23.2 %collective-permute-start.22 = (f32[4,10,3,70]{3,2,1,0:T(4,128)S(1)}, f32[4,10,3,70]{3,2,1,0:T(4,128)S(1)}, u32[]{:S(2)}, u32[]{:S(2)}) collective-permute-start(f32[4,10,3,70]{3,2,1,0:T(4,128)S(1)} %get-tuple-element.46), channel_id=1, source_target_pairs={{0,1},{1,2},{2,3},{4,5},{5,6},{6,7},{8,9},{9,10},{10,11},{12,13},{... | collective-permute-start | bytes 100808 | tf_op jit(solution)/shard_map/ppermute | solution.py:40
  222.9 29.2 %collective-permute-start.29 = (f32[3,8,1,128]{3,2,1,0:T(1,128)S(1)}, f32[3,8,1,128]{3,2,1,0:T(1,128)S(1)}, u32[]{:S(2)}, u32[]{:S(2)}) collective-permute-start(f32[3,8,1,128]{3,2,1,0:T(1,128)S(1)} %get-tuple-element.23), channel_id=1, source_target_pairs={{0,1},{1,2},{2,3},{4,5},{5,6},{6,7},{8,9},{9,10},{10,11},{12,13},{... | collective-permute-start | bytes 36872 | tf_op jit(solution)/shard_map/ppermute | solution.py:23
  236.1 9.2 %collective-permute-start.26 = (f32[3,1,16,128]{3,2,1,0:T(8,128)S(1)}, f32[3,1,16,128]{3,2,1,0:T(8,128)S(1)}, u32[]{:S(2)}, u32[]{:S(2)}) collective-permute-start(f32[3,1,16,128]{3,2,1,0:T(8,128)S(1)} %get-tuple-element.25), channel_id=1, source_target_pairs={{4,0},{8,4},{12,8},{16,12},{20,16},{24,20},{28,24},{32,28},{36,32}... | collective-permute-start | bytes 73736 | tf_op jit(solution)/shard_map/ppermute | solution.py:24
  238.0 11.0 %collective-permute-start.27 = (f32[3,1,16,128]{3,2,1,0:T(8,128)S(1)}, f32[3,1,16,128]{3,2,1,0:T(8,128)S(1)}, u32[]{:S(2)}, u32[]{:S(2)}) collective-permute-start(f32[3,1,16,128]{3,2,1,0:T(8,128)S(1)} %get-tuple-element.24), channel_id=1, source_target_pairs={{0,4},{4,8},{8,12},{12,16},{16,20},{20,24},{24,28},{28,32},{32,36}... | collective-permute-start | bytes 73736 | tf_op jit(solution)/shard_map/ppermute | solution.py:23
  241.9 14.3 %collective-permute-start.28 = (f32[3,8,1,128]{3,2,1,0:T(1,128)S(1)}, f32[3,8,1,128]{3,2,1,0:T(1,128)S(1)}, u32[]{:S(2)}, u32[]{:S(2)}) collective-permute-start(f32[3,8,1,128]{3,2,1,0:T(1,128)S(1)} %get-tuple-element.22), channel_id=1, source_target_pairs={{1,0},{2,1},{3,2},{5,4},{6,5},{7,6},{9,8},{10,9},{11,10},{13,12},{... | collective-permute-start | bytes 36872 | tf_op jit(solution)/shard_map/ppermute | solution.py:24
  (10 other events, 99.1 us)
where the time goes:
time: 267 us; the launch traced here: 266 us
  starting transfers between devices  138 us (52%)
  waiting for transfers between devices  64.8 us (24%)
  local copies, waits for them, and re-layouts  48.6 us (18%)
  other arithmetic  13.7 us (5%)
    ppermute x12, starting transfers between devices, extended_2(): lax.ppermute(last, axis, up)  61.5 us
    ppermute x12, starting transfers between devices, extended_2(): lax.ppermute(first, axis, [(b, a) for a, b in up])  36.5 us
    ppermute x12, waiting for transfers between devices, extended_2(): lax.ppermute(first, axis, [(b, a) for a, b in up])  35.4 us
    ppermute x3, starting transfers between devices, padded_2(): lax.ppermute(lax.slice_in_dim(block, block.shape[dim] - width, None, axis...  17.6 us
    ppermute x3, waiting for transfers between devices, padded_2(): lax.ppermute(lax.slice_in_dim(block, block.shape[dim] - width, None, axis...  16.5 us
    reshape x1, local copies, waits for them, and re-layouts, block_mean(): field.reshape(components, size_x // 2, 2, size_y // 2, 2, size_z // 2, 2)  14 us
    all_to_all x1, starting transfers between devices, on_device(): lax.all_to_all(velocity_prev, 'gx', split_axis=3, concat_axis=1, tiled=True)  12.8 us
    ppermute x12, waiting for transfers between devices, extended_2(): lax.ppermute(last, axis, up)  10.3 us
  transfers between devices with their start and end apart: 31, of which 12 were waited for; matrix products, arithmetic and copies ran while one was open for 20% of the time, Pallas kernels for 0%

commit v1 on v0

v1 whole, which is shorter than its diff:
```python
import functools

import jax
import jax.numpy as jnp
import numpy as np
from jax import lax
from jax.experimental import pallas as pl
from jax.experimental.pallas import tpu as pltpu
from jax.sharding import PartitionSpec as P

SWEEPS = 2
COARSE_SWEEPS = 4
LX = 5
damping = 0.8
keep = 1.0 - damping
root_half = 0.7071067811865476
MESH = pl.DeviceIdType.MESH
F32 = jnp.float32

X1, Z1, Y1, Y2, X2, XE, Z2, X3, Z3, DZ, DX, DY, BZ, BX, BY, COUNT = range(16)


def haar_matrix(devices):
    size = 4 * devices
    approx = np.eye(size)
    details = []
    for _ in range(LX - 1):
        even, odd = approx[:, 0::2], approx[:, 1::2]
        approx, detail = (even + odd) * root_half, (even - odd) * root_half
        details.append(detail)
    whole = np.concatenate([approx] + details[::-1], axis=1)
    parts = whole.reshape(devices, 4, size)
    return np.concatenate([parts[:, m] for m in range(4)], axis=1).astype(np.float32)


def dot(a, b, dims=((1,), (0,))):
    return lax.dot_general(
        a, b, (dims, ((), ())), precision=lax.Precision.HIGHEST, preferred_element_type=F32
    )


def lanes(shape):
    return lax.broadcasted_iota(jnp.int32, shape, len(shape) - 1)


def rows(shape):
    return lax.broadcasted_iota(jnp.int32, shape, len(shape) - 2)


def kernel(
    sizes, vp, f, r, mcat, vel, comp,
    c_ref, u1, u2, gb, tp, uh1, uh2, sendt, recvt,
    xs, xr1, xr2, xr3, xes, xer, zs1, zr1, zs2, zr2, zs3, zr3,
    y1s, y1r, y2s, y2r,
    down, dzr, dext, dxr, dys, dyr, dds, ddr,
    bown, bzr, bext, bxr, bys, byr, bds, bdr,
    ddiag, cdext, cf, cz, eu, ph,
    ssem, rsem, dssem, drsem, assem, arsem,
):
    n_agg, n_gx, n_gy = sizes
    per = 128 // n_gx
    axes = {"agg": n_agg, "gx": n_gx, "gy": n_gy}
    here = {name: lax.axis_index(name) for name in axes}

    def wrap(name, step):
        return lax.rem(here[name] + step + axes[name], axes[name])

    for ref in (xr1, xr2, xr3, xer, zr1, zr2, zr3, y1r, y2r, dzr, dxr, dyr, ddr, bzr, bxr, byr, bdr):
        ref[...] = jnp.zeros(ref.shape, F32)

    barrier = pltpu.get_barrier_semaphore()

    def greet(step, carry):
        pl.semaphore_signal(
            barrier, inc=1, device_id={"gx": lax.rem(here["gx"] + step, n_gx)}, device_id_type=MESH
        )
        return carry

    lax.fori_loop(1, n_gx, greet, 0)
    for name in ("gy", "agg"):
        for step in (1, -1):
            pl.semaphore_signal(barrier, inc=1, device_id={name: wrap(name, step)}, device_id_type=MESH)
    for sx in (1, -1):
        for sy in (1, -1):
            pl.semaphore_signal(
                barrier, inc=1, device_id={"gx": wrap("gx", sx), "gy": wrap("gy", sy)}, device_id_type=MESH
            )

    def pair_copy(message, axis, src, dst, side):
        step = 1 if side == 0 else -1
        return pltpu.make_async_remote_copy(
            src_ref=src.at[side], dst_ref=dst.at[side],
            send_sem=ssem.at[message, side], recv_sem=rsem.at[message, side],
            device_id={axis: here[axis] + step}, device_id_type=MESH,
        )

    def whole_copy(message, axis, src, dst, side):
        step = 1 if side == 0 else -1
        return pltpu.make_async_remote_copy(
            src_ref=src, dst_ref=dst.at[side],
            send_sem=ssem.at[message, side], recv_sem=rsem.at[message, side],
            device_id={axis: here[axis] + step}, device_id_type=MESH,
        )

    ends = []

    def start(message, axis, src, dst, make=pair_copy):
        @pl.when(here[axis] < axes[axis] - 1)
        def _():
            make(message, axis, src, dst, 0).start()

        @pl.when(here[axis] > 0)
        def _():
            make(message, axis, src, dst, 1).start()

        ends.append((message, axis, src, dst, make))

    def arrive(message, axis, src, dst, make=pair_copy):
        @pl.when(here[axis] > 0)
        def _():
            make(message, axis, src, dst, 0).wait_recv()

        @pl.when(here[axis] < axes[axis] - 1)
        def _():
            make(message, axis, src, dst, 1).wait_recv()

    def corner_copy(kind, src, dst, xs_, ys_):
        sx, sy = 1 if xs_ == 0 else -1, 1 if ys_ == 0 else -1
        k = xs_ * 2 + ys_
        return pltpu.make_async_remote_copy(
            src_ref=src.at[k], dst_ref=dst.at[k],
            send_sem=dssem.at[kind, k], recv_sem=drsem.at[kind, k],
            device_id={"gx": here["gx"] + sx, "gy": here["gy"] + sy}, device_id_type=MESH,
        )

    def has(axis, side):
        return here[axis] < axes[axis] - 1 if side == 0 else here[axis] > 0

    def from_(axis, side):
        return here[axis] > 0 if side == 0 else here[axis] < axes[axis] - 1

    def corners(kind, src, dst, verb):
        for xs_ in (0, 1):
            for ys_ in (0, 1):
                test = from_ if verb == "recv" else has

                @pl.when(jnp.logical_and(test("gx", xs_), test("gy", ys_)))
                def _(xs_=xs_, ys_=ys_):
                    copy = corner_copy(kind, src, dst, xs_, ys_)
                    if verb == "start":
                        copy.start()
                    elif verb == "recv":
                        copy.wait_recv()
                    else:
                        copy.wait_send()

    lane8, lane16, lane128 = lanes((8, 128)), lanes((16, 128)), lanes((128, 128))
    sub8 = rows((8, 128))
    y_at = lax.rem(rows((128, 128)), 16)

    def comp_of(ref, c):
        return ref[c * 128 : (c + 1) * 128, :]

    def plane(ref, c, j):
        return ref[pl.ds(c * 128 + j, 8, stride=16), :]

    def put_plane(ref, c, j, value):
        ref[pl.ds(c * 128 + j, 8, stride=16), :] = value

    def z_pack(tiles, column, lane):
        packed = jnp.zeros(lane.shape, F32)
        for place, tile in enumerate(tiles):
            packed = jnp.where(lane == place, pltpu.roll(tile, (place - column) % 128, 1), packed)
        return packed

    def z_tiles(ref):
        return [ref[t * 16 : (t + 1) * 16, :] for t in range(24)]

    def x_stage(ref):
        for c in range(3):
            xs_value = ref[c * 128 + 112 : c * 128 + 128, :]
            xs[stage, 0, c] = xs_value
            xs[stage, 1, c] = ref[c * 128 : c * 128 + 16, :]

    def spread(packed, c, lane_at):
        return jnp.concatenate(
            [pltpu.roll(packed, (lane_at - (c * 8 + x)) % 128, 1) for x in range(8)], axis=0
        )

    def around(u, x_low, x_high, z_low, z_high):
        total = jnp.concatenate([x_low, u[:112]], axis=0) + jnp.concatenate([u[16:], x_high], axis=0)
        total = total + jnp.where(lane128 == 0, z_low, pltpu.roll(u, 1, 1))
        total = total + jnp.where(lane128 == 127, z_high, pltpu.roll(u, 127, 1))
        total = total + jnp.where(y_at == 0, 0.0, pltpu.roll(u, 1, 0))
        return total + jnp.where(y_at == 15, 0.0, pltpu.roll(u, 127, 0))

    reaction = r[...]
    c_ref[...] = damping / (6.0 + reaction)
    for c in range(3):
        for side, j in ((0, 15), (1, 0)):
            y1s[side, c] = plane(vp, c, j)
    for side, j in ((0, 15), (1, 0)):
        y1s[side, 3] = c_ref[pl.ds(j, 8, stride=16), :]
    stage = 0
    x_stage(vp)
    zs1[0] = z_pack(z_tiles(vp), 127, lane16)
    zs1[1] = z_pack(z_tiles(vp), 0, lane16)

    halves = jnp.where(lax.shift_right_logical(rows((128, 128)), 1) == lane128, 0.125, 0.0)
    pairs = reaction.reshape(4, 2, 16, 128)
    tp[0:64, :] = (pairs[:, 0] + pairs[:, 1]).reshape(64, 128)
    mean_r = dot(tp[pl.ds(0, 32, stride=2), :] + tp[pl.ds(1, 32, stride=2), :], halves)
    inverse = damping / ((6.0 + 4.0 * mean_r) * 0.25)
    down[...] = jnp.where(lanes((32, 128)) < 64, inverse, 0.0).reshape(4, 8, 128)

    row192 = rows((192, 128))
    first = []
    for c in range(3):
        both = comp_of(vp, c).reshape(4, 2, 16, 128)
        first.append(((both[:, 0] + both[:, 1]) * root_half).reshape(64, 128))
    a1 = jnp.concatenate(first, axis=0)
    even = lax.rem(row192, 2) == 0
    a1 = jnp.where(even, a1 + pltpu.roll(a1, 191, 0), pltpu.roll(a1, 1, 0) - a1) * root_half
    out_z, in_z = rows((128, 128)), lane128
    same = lax.shift_right_logical(out_z, 1) == lax.shift_right_logical(in_z, 1)
    minus = jnp.logical_and(lax.rem(out_z, 2) == 1, lax.rem(in_z, 2) == 1)
    pass_z = jnp.where(same, jnp.where(minus, -root_half, root_half), 0.0).astype(F32)
    turned = jnp.concatenate([dot(pass_z, a1, ((1,), (1,))), jnp.zeros((128, 64), F32)], axis=1)
    for t in range(n_gx):
        sendt[t] = turned[t * per : (t + 1) * per, :]

    pl.semaphore_wait(barrier, n_gx - 1 + 8)

    start(Y1, "gy", y1s, y1r)
    start(X1, "gx", xs.at[0], xr1)
    start(Z1, "agg", zs1, zr1)
    start(DZ, "agg", down, dzr, whole_copy)
    arrive(X1, "gx", xs.at[0], xr1)
    arrive(Z1, "agg", zs1, zr1)
    z_low, z_high = zr1[0], zr1[1]
    for c in range(3):
        u = comp_of(vp, c)
        total = comp_of(f, c) + around(
            u, xr1[0, c], xr1[1, c], spread(z_low, c, 0), spread(z_high, c, 127)
        )
        gb[c * 128 : (c + 1) * 128, :] = total
        u1[c * 128 : (c + 1) * 128, :] = keep * u + c_ref[...] * total
    for c in range(3):
        for side, j, inner in ((0, 15, 14), (1, 0, 1)):
            y2s[side, c] = plane(gb, c, j)
            y2s[side, 3 + c] = plane(f, c, j) + plane(u1, c, inner)
    start(Y2, "gy", y2s, y2r)

    def widen(own, received, wide, n):
        lane = lanes((n * 8, 128))
        mine = own[...].reshape(n * 8, 128)
        low, high = received[0].reshape(n * 8, 128), received[1].reshape(n * 8, 128)
        turned_ = pltpu.roll(jnp.where(lane < 32, high, low), 64, 1)
        edge = jnp.logical_or(lane < 68, lane >= 124)
        value = jnp.where(lane < 64, mine, jnp.where(edge, turned_, 0.0))
        wide[...] = value.reshape(n, 8, 128)

    def stage_rows(wide, y_stage, corner_stage, n):
        for c in range(n):
            for half in range(2):
                a, b = wide[c * 4 + 2 * half], wide[c * 4 + 2 * half + 1]
                y_stage[0, c * 2 + half] = jnp.where(sub8 < 4, pltpu.roll(a, 4, 0), b)
                y_stage[1, c * 2 + half] = jnp.where(sub8 < 4, a, pltpu.roll(b, 4, 0))
            for xs_ in (0, 1):
                order = (3, 2, 1) if xs_ == 0 else (0, 1, 2)
                one, two, three = (wide[c * 4 + i] for i in order)
                corner_stage[xs_ * 2, c] = jnp.where(
                    sub8 >= 4, one, jnp.where(sub8 >= 2, pltpu.roll(two, 4, 0), pltpu.roll(three, 1, 0))
                )
                corner_stage[xs_ * 2 + 1, c] = jnp.where(
                    sub8 < 4, one, jnp.where(sub8 < 6, pltpu.roll(two, 4, 0), pltpu.roll(three, 7, 0))
                )

    def assemble(wide, x_got, y_got, corner_got, c):
        tiles = []
        for place in range(12):
            if 4 <= place < 8:
                i = place - 4
                main = wide[c * 4 + i]
                high, low = y_got[1, c * 2 + i // 2], y_got[0, c * 2 + i // 2]
                if i % 2 == 0:
                    halo = jnp.where(sub8 < 4, high, pltpu.roll(low, 4, 0))
                else:
                    halo = jnp.where(sub8 < 4, pltpu.roll(high, 4, 0), low)
            else:
                side = 0 if place < 4 else 1
                away = 4 - place if side == 0 else place - 7
                main = x_got[side, c * 4 + (place if side == 0 else place - 8)]
                if away == 4:
                    halo = jnp.zeros((8, 128), F32)
                else:
                    low, high = corner_got[side * 2, c], corner_got[side * 2 + 1, c]
                    if away == 1:
                        halo = jnp.where(sub8 < 4, high, low)
                    elif away == 2:
                        halo = jnp.where(
                            sub8 < 2, pltpu.roll(high, 4, 0),
                            jnp.where(sub8 >= 6, pltpu.roll(low, 4, 0), 0.0),
                        )
                    else:
                        halo = jnp.where(
                            sub8 == 0, pltpu.roll(high, 1, 0),
                            jnp.where(sub8 == 7, pltpu.roll(low, 7, 0), 0.0),
                        )
            tiles += [main, halo]
        return jnp.concatenate(tiles, axis=0)

    arrive(DZ, "agg", down, dzr, whole_copy)
    widen(down, dzr, dext, 4)
    stage_rows(dext, dys, dds, 1)
    start(DX, "gx", dext, dxr, whole_copy)
    start(DY, "gy", dys, dyr)
    corners(0, dds, ddr, "start")

    arrive(Y1, "gy", y1s, y1r)
    for c in range(3):
        for side, j in ((0, 0), (1, 15)):
            put_plane(u1, c, j, plane(u1, c, j) + c_ref[pl.ds(j, 8, stride=16), :] * y1r[side, c])
    arrive(Y2, "gy", y2s, y2r)
    for c in range(3):
        for side, j in ((0, 0), (1, 15)):
            at = (side * 3 + c) * 8
            uh1[at : at + 8, :] = keep * y1r[side, c] + y1r[side, 3] * (y2r[side, c] + plane(vp, c, j))

    stage = 1
    x_stage(u1)
    xes[0, 0:6, :] = uh1[pl.ds(7, 6, stride=8), :]
    xes[1, 0:6, :] = uh1[pl.ds(0, 6, stride=8), :]
    start(X2, "gx", xs.at[1], xr2)
    start(XE, "gx", xes, xer)
    edge_tiles = [uh1[t * 8 : (t + 1) * 8, :] for t in range(6)]
    zs2[0, 0:16, :] = z_pack(z_tiles(u1), 127, lane16)
    zs2[0, 16:24, :] = z_pack(edge_tiles, 127, lane8)
    zs2[1, 0:16, :] = z_pack(z_tiles(u1), 0, lane16)
    zs2[1, 16:24, :] = z_pack(edge_tiles, 0, lane8)
    start(Z2, "agg", zs2, zr2)

    def line_copy(step):
        target = lax.rem(here["gx"] + step, n_gx)
        return pltpu.make_async_remote_copy(
            src_ref=sendt.at[target], dst_ref=recvt.at[here["gx"]],
            send_sem=assem, recv_sem=arsem, device_id={"gx": target}, device_id_type=MESH,
        )

    def send_line(step, carry):
        line_copy(step).start()
        return carry

    lax.fori_loop(1, n_gx, send_line, 0)

    arrive(X2, "gx", xs.at[1], xr2)
    arrive(XE, "gx", xes, xer)
    arrive(Z2, "agg", zs2, zr2)
    z_low, z_high = zr2[0, 0:16, :], zr2[1, 0:16, :]
    for c in range(3):
        u = comp_of(u1, c)
        total = comp_of(f, c) + around(
            u, xr2[0, c], xr2[1, c], spread(z_low, c, 0), spread(z_high, c, 127)
        )
        u2[c * 128 : (c + 1) * 128, :] = keep * u + c_ref[...] * total
    edge_low, edge_high = zr2[0, 16:24, :], zr2[1, 16:24, :]
    for c in range(3):
        for side, j in ((0, 0), (1, 15)):
            k = side * 3 + c
            at = k * 8
            p = uh1[at : at + 8, :]
            put_plane(u2, c, j, plane(u2, c, j) + c_ref[pl.ds(j, 8, stride=16), :] * p)
            near = jnp.where(sub8 == 0, xer[0, k : k + 1, :], pltpu.roll(p, 1, 0))
            near = near + jnp.where(sub8 == 7, xer[1, k : k + 1, :], pltpu.roll(p, 7, 0))
            near = near + jnp.where(lane8 == 0, pltpu.roll(edge_low, (-k) % 128, 1), pltpu.roll(p, 1, 1))
            near = near + jnp.where(
                lane8 == 127, pltpu.roll(edge_high, 127 - k, 1), pltpu.roll(p, 127, 1)
            )
            uh2[at : at + 8, :] = keep * p + y1r[side, 3] * (y2r[side, 3 + c] + near + plane(u1, c, j))

    stage = 2
    x_stage(u2)
    start(X3, "gx", xs.at[2], xr3)
    zs3[0] = z_pack(z_tiles(u2), 127, lane16)
    zs3[1] = z_pack(z_tiles(u2), 0, lane16)
    start(Z3, "agg", zs3, zr3)

    arrive(DX, "gx", dext, dxr, whole_copy)
    arrive(DY, "gy", dys, dyr)
    corners(0, dds, ddr, "recv")
    cdext[...] = assemble(dext, dxr, dyr, ddr, 0)

    arrive(X3, "gx", xs.at[2], xr3)
    arrive(Z3, "agg", zs3, zr3)
    z_low, z_high = zr3[0], zr3[1]
    for c in range(3):
        u = comp_of(u2, c)
        gb[c * 128 : (c + 1) * 128, :] = (
            comp_of(f, c) - (6.0 + r[...]) * u
            + around(u, xr3[0, c], xr3[1, c], spread(z_low, c, 0), spread(z_high, c, 127))
        )
    for c in range(3):
        for side, j in ((0, 0), (1, 15)):
            at = (side * 3 + c) * 8
            put_plane(gb, c, j, plane(gb, c, j) + uh2[at : at + 8, :])
    for c in range(3):
        both = comp_of(gb, c).reshape(4, 2, 16, 128)
        tp[c * 64 : (c + 1) * 64, :] = (both[:, 0] + both[:, 1]).reshape(64, 128)
    rhs = dot(tp[pl.ds(0, 96, stride=2), :] + tp[pl.ds(1, 96, stride=2), :], halves)
    bown[...] = rhs.reshape(12, 8, 128)
    start(BZ, "agg", bown, bzr, whole_copy)
    arrive(BZ, "agg", bown, bzr, whole_copy)
    widen(bown, bzr, bext, 12)
    stage_rows(bext, bys, bds, 3)
    start(BY, "gy", bys, byr)
    corners(1, bds, bdr, "start")
    start(BX, "gx", bext, bxr, whole_copy)

    many = n_gx - 1
    lines = pltpu.make_async_remote_copy(
        src_ref=sendt.at[pl.ds(0, many)], dst_ref=recvt.at[pl.ds(0, many)],
        send_sem=assem, recv_sem=arsem, device_id={"gx": wrap("gx", 1)}, device_id_type=MESH,
    )
    lines.wait_recv()
    lines.wait_send()
    recvt[here["gx"]] = sendt[here["gx"]]
    for k in range(per):
        got = recvt[:, k, :]
        wide = dot(got[:, 0:192], mcat[...], ((0,), (0,)))
        for c in range(3):
            value = 0.0
            for m in range(4):
                at = (c * 4 + m) * 16
                value = value + wide[at : at + 16, m * 4 * n_gx : (m + 1) * 4 * n_gx]
            comp[k, c] = value

    arrive(BX, "gx", bext, bxr, whole_copy)
    arrive(BY, "gy", bys, byr)
    corners(1, bds, bdr, "recv")

    y16 = lax.rem(rows((192, 128)), 16)
    fine = lane128 // 2 == rows((128, 128))
    beyond = jnp.logical_or(
        jnp.logical_and(lane128 == 0, rows((128, 128)) == 127),
        jnp.logical_and(lane128 == 127, rows((128, 128)) == 64),
    )
    up = jnp.concatenate([jnp.where(fine, 1.0, 0.0), jnp.where(beyond, 1.0, 0.0)], axis=1).astype(F32)
    none = jnp.zeros((16, 128), F32)
    for c in range(3):
        rhs_c = assemble(bext, bxr, byr, bdr, c)
        weight = cdext[...]
        e = weight * rhs_c
        for _ in range(COARSE_SWEEPS - 1):
            near = jnp.concatenate([none, e[:176]], axis=0) + jnp.concatenate([e[16:], none], axis=0)
            near = near + pltpu.roll(e, 1, 1) + pltpu.roll(e, 127, 1)
            near = near + jnp.where(y16 == 0, pltpu.roll(e, 192 - 15, 0), pltpu.roll(e, 1, 0))
            near = near + jnp.where(y16 == 15, pltpu.roll(e, 15, 0), pltpu.roll(e, 191, 0))
            e = keep * e + weight * (rhs_c + 0.25 * near)
        refined = dot(e[48:144], up)
        eu[c * 96 : (c + 1) * 96, :] = refined[:, 0:128]
        for ref, part in ((cf, refined[:, 0:128]), (cz, refined[:, 128:256])):
            main = part.reshape(6, 16, 128)[:, 0:8].reshape(48, 128)
            ref[pl.ds(c * 96, 48, stride=2), :] = main
            ref[pl.ds(c * 96 + 1, 48, stride=2), :] = main
        for side, row in ((0, 15), (1, 8)):
            line = eu[pl.ds(c * 96 + 16 + row, 4, stride=16), :]
            at = (side * 3 + c) * 8
            ph[pl.ds(at, 4, stride=2), :] = line
            ph[pl.ds(at + 1, 4, stride=2), :] = line

    def doubled(ref, c):
        value = ref[c * 96 + 16 : c * 96 + 80, :].reshape(4, 1, 16, 128)
        return jnp.broadcast_to(value, (4, 2, 16, 128)).reshape(128, 128)

    for c in range(3):
        w = comp_of(u2, c) + doubled(cf, c)
        beside = doubled(cz, c)
        total = comp_of(f, c) + around(
            w,
            xr3[0, c] + cf[c * 96 : c * 96 + 16, :],
            xr3[1, c] + cf[c * 96 + 80 : c * 96 + 96, :],
            spread(z_low, c, 0) + beside,
            spread(z_high, c, 127) + beside,
        )
        vel[c * 128 : (c + 1) * 128, :] = keep * w + c_ref[...] * total
    for c in range(3):
        for side, j in ((0, 0), (1, 15)):
            at = (side * 3 + c) * 8
            beyond_y = uh2[at : at + 8, :] + ph[at : at + 8, :]
            put_plane(vel, c, j, plane(vel, c, j) + c_ref[pl.ds(j, 8, stride=16), :] * beyond_y)

    for message, axis, src, dst, make in ends:

        @pl.when(here[axis] < axes[axis] - 1)
        def _(args=(message, axis, src, dst), make=make):
            make(*args, 0).wait_send()

        @pl.when(here[axis] > 0)
        def _(args=(message, axis, src, dst), make=make):
            make(*args, 1).wait_send()

    corners(0, dds, ddr, "send")
    corners(1, bds, bdr, "send")


def on_device(sizes, velocity_prev, forcing, reaction):
    n_agg, n_gx, n_gy = sizes
    per = 128 // n_gx
    v = pltpu.VMEM
    scratch = [
        v((128, 128), F32), v((384, 128), F32), v((384, 128), F32), v((384, 128), F32),
        v((192, 128), F32), v((48, 128), F32), v((48, 128), F32),
        v((n_gx, per, 256), F32), v((n_gx, per, 256), F32),
        v((3, 2, 3, 16, 128), F32), v((2, 3, 16, 128), F32), v((2, 3, 16, 128), F32), v((2, 3, 16, 128), F32),
        v((2, 8, 128), F32), v((2, 8, 128), F32),
        v((2, 16, 128), F32), v((2, 16, 128), F32), v((2, 24, 128), F32), v((2, 24, 128), F32),
        v((2, 16, 128), F32), v((2, 16, 128), F32),
        v((2, 4, 8, 128), F32), v((2, 4, 8, 128), F32), v((2, 6, 8, 128), F32), v((2, 6, 8, 128), F32),
    ]
    for n in (1, 3):
        scratch += [
            v((n * 4, 8, 128), F32), v((2, n * 4, 8, 128), F32), v((n * 4, 8, 128), F32),
            v((2, n * 4, 8, 128), F32), v((2, n * 2, 8, 128), F32), v((2, n * 2, 8, 128), F32),
            v((4, n, 8, 128), F32), v((4, n, 8, 128), F32),
        ]
    scratch += [
        v((8, 128), F32), v((192, 128), F32), v((288, 128), F32), v((288, 128), F32), v((288, 128), F32),
        v((48, 128), F32),
        pltpu.SemaphoreType.DMA((COUNT, 2)), pltpu.SemaphoreType.DMA((COUNT, 2)),
        pltpu.SemaphoreType.DMA((2, 4)), pltpu.SemaphoreType.DMA((2, 4)),
        pltpu.SemaphoreType.DMA, pltpu.SemaphoreType.DMA,
    ]
    vmem = pl.BlockSpec(memory_space=pltpu.VMEM)
    velocity, compressed = pl.pallas_call(
        functools.partial(kernel, sizes),
        out_shape=(
            jax.ShapeDtypeStruct((384, 128), F32),
            jax.ShapeDtypeStruct((per, 3, 16, 4 * n_gx), F32),
        ),
        in_specs=[vmem] * 4,
        out_specs=(vmem, vmem),
        scratch_shapes=scratch,
        compiler_params=pltpu.CompilerParams(collective_id=0, has_side_effects=True),
        name="vcycle",
    )(
        velocity_prev.reshape(384, 128), forcing.reshape(384, 128), reaction.reshape(128, 128),
        jnp.asarray(haar_matrix(n_gx)),
    )
    return velocity.reshape(3, 8, 16, 128), jnp.transpose(compressed, (1, 2, 0, 3))


def solution(mesh):
    placed = (P(None, "gx", "gy", "agg"), P(None, "gx", "gy", "agg"), P("gx", "gy", "agg"))
    sizes = tuple(mesh.shape[name] for name in ("agg", "gx", "gy"))
    return jax.shard_map(
        functools.partial(on_device, sizes),
        mesh=mesh,
        in_specs=placed,
        out_specs=(P(None, "gx", "gy", "agg"), P(None, "gy", ("agg", "gx"), None)),
        check_vma=False,
    )
```

time: 267 us -> 72 us (0.27)
  the two profiles are of different devices: /device:TPU:232 before, /device:TPU:15 now
where the time goes in v1:
time: 72 us; the launch traced here: 71.8 us
  Pallas kernels  68.8 us (96%)
  local copies, waits for them, and re-layouts  2.29 us (3%)
    pallas_call x1, Pallas kernels, on_device(): pl.pallas_call(functools.partial(kernel, sizes), out_shape=(jax.ShapeDtyp...  68.8 us
    unnamed x4, local copies, waits for them, and re-layouts  2.29 us

profile of v1, /device:TPU:15, one launch (start us, length us, event | category | flops | bytes accessed | tf_op | source)
XLA Modules:
  0.0 71.8 jit_solution(10903180623089323159)
XLA Ops:
  0.6 68.8 %vcycle.1 = (f32[384,128]{1,0:T(8,128)}, f32[4,3,16,128]{3,2,1,0:T(8,128)}) custom-call(f32[384,128]{1,0:T(8,128)} %bitcast.6, f32[384,128]{1,0:T(8,128)} %bitcast.7, f32[128,128]{1,0:T(8,128)} %bitcast.9, f32[32,512]{1,0:T(8,128)} %constant.2.clone.mcat), custom_call_target="tpu_custom_call" | custom-call | tf_op jit(solution)/shard_map/vcycle/pallas_call | solution.py:534
  69.5 0.0 copy-start
  69.5 1.6 %copy.6 = f32[3,16,4,128]{3,2,1,0:T(4,128)} copy(f32[3,16,4,128]{3,1,0,2:T(8,128)} %bitcast.8) | data formatting | bytes 196608
  71.1 0.0 copy-done
  71.1 0.7 copy.8
Async XLA Ops:
  69.5 1.6 %copy-start = (f32[384,128]{1,0:T(8,128)S(1)}, f32[384,128]{1,0:T(8,128)}, u32[]{:S(2)}) copy-start(f32[384,128]{1,0:T(8,128)} %get-tuple-element.4) | copy-start | bytes 589828

commit v2 on v0

v2 whole, which is shorter than its diff:
```python
import functools

import jax
import jax.numpy as jnp
import numpy as np
from jax import lax
from jax.experimental import pallas as pl
from jax.experimental.pallas import tpu as pltpu
from jax.sharding import PartitionSpec as P

SWEEPS = 2
COARSE_SWEEPS = 4
LX = 5
damping = 0.8
keep = 1.0 - damping
root_half = 0.7071067811865476
MESH = pl.DeviceIdType.MESH
F32 = jnp.float32

X1, Z1, X2, Z2, X3, Z3, XF2, ZF2, XF3, ZF3, DZ, DX, DXZ, BZ, BX, BXZ, Y1, Y2, Y3, Y4, COUNT = range(21)
ROW = 4
TURNS = (1, 1, 2, 2, 3, 3, 4, 5)

def haar_matrix(devices):
    size = 4 * devices
    approx = np.eye(size)
    details = []
    for _ in range(LX - 1):
        even, odd = approx[:, 0::2], approx[:, 1::2]
        approx, detail = (even + odd) * root_half, (even - odd) * root_half
        details.append(detail)
    whole = np.concatenate([approx] + details[::-1], axis=1)
    parts = whole.reshape(devices, 4, size)
    return np.concatenate([parts[:, m] for m in range(4)], axis=1).astype(np.float32)


def dot(a, b, dims=((1,), (0,))):
    return lax.dot_general(
        a, b, (dims, ((), ())), precision=lax.Precision.HIGHEST, preferred_element_type=F32
    )


def lanes(shape):
    return lax.broadcasted_iota(jnp.int32, shape, len(shape) - 1)


def rows(shape):
    return lax.broadcasted_iota(jnp.int32, shape, len(shape) - 2)


def kernel(
    sizes, vp_in, f_in, r_in, m_in, vel, comp,
    vp, f, r, mcat, c_ref, u1, u2, uz, gb, tp, sendt, recvt,
    xs, xr1, xr2, xr3, zs1, zr1, zs2, zr2, zs3, zr3,
    p1, p2, ps, xf2s, xf2r, zf2s, zf2r, xf3s, xf3r, zf3s, zf3r,
    y1s, y1r, y2s, y2r, y3s, y3r, y4s, y4r,
    down, dtile, dpack, dxr, dzs, dzr, dxz, bown, btile, bpack, bxr, bzs, bzr, bxz,
    cdext, cf, cz, eu, ph,
    insem, ssem, rsem, assem, arsem, ready, token_up, token_down,
):
    n_agg, n_gx, n_gy = sizes
    per = 128 // n_gx
    levels = n_gx // ROW
    axes = {"agg": n_agg, "gx": n_gx, "gy": n_gy}
    here = {name: lax.axis_index(name) for name in axes}
    gx = here["gx"]
    level, place_x = gx // ROW, lax.rem(gx, ROW)

    def upper(axis):
        return here[axis] < axes[axis] - 1

    def lower(axis):
        return here[axis] > 0

    for ref in (
        xr1, xr2, xr3, zr1, zr2, zr3, xf2r, zf2r, xf3r, zf3r, y1r, y2r, y3r, y4r, dzr, dxr, dxz, bzr, bxr, bxz
    ):
        ref[...] = jnp.zeros(ref.shape, F32)

    barrier = pltpu.get_barrier_semaphore()

    def greet(test, device):
        @pl.when(test)
        def _():
            pl.semaphore_signal(barrier, inc=1, device_id=device, device_id_type=MESH)

    crossing_up = jnp.logical_and(place_x == ROW - 1, upper("gx"))
    crossing_down = jnp.logical_and(place_x == 0, lower("gx"))
    greet(upper("gy"), {"gy": here["gy"] + 1})
    greet(upper("agg"), {"agg": here["agg"] + 1})
    greet(lower("agg"), {"agg": here["agg"] - 1})
    for step in range(1, ROW):
        pl.semaphore_signal(
            barrier, inc=1, device_id={"gx": level * ROW + lax.rem(place_x + step, ROW)}, device_id_type=MESH
        )
    greet(crossing_up, {"gx": gx + 1})
    greet(crossing_down, {"gx": gx - 1})
    greet(level < levels - 1, {"gx": gx + ROW})
    greet(level > 0, {"gx": gx - ROW})

    fetches = [
        pltpu.make_async_copy(source, ref, insem.at[k])
        for k, (source, ref) in enumerate(((vp_in, vp), (r_in, r), (f_in, f), (m_in, mcat)))
    ]
    for fetch in fetches:
        fetch.start()

    def one_copy(message, axis, src, dst, side):
        step = 1 if side == 0 else -1
        return pltpu.make_async_remote_copy(
            src_ref=src[side], dst_ref=dst.at[side],
            send_sem=ssem.at[message, side], recv_sem=rsem.at[message, side],
            device_id={axis: here[axis] + step}, device_id_type=MESH,
        )

    ends = []

    def start(message, axis, src, dst, sides=(0, 1)):
        for side in sides:

            @pl.when(upper(axis) if side == 0 else lower(axis))
            def _(side=side):
                one_copy(message, axis, src, dst, side).start()

            ends.append((message, axis, src, dst, side))

    def arrive(message, axis, src, dst):
        for side in (0, 1):

            @pl.when(lower(axis) if side == 0 else upper(axis))
            def _(side=side):
                one_copy(message, axis, src, dst, side).wait_recv()

    def both(ref):
        return (ref.at[0], ref.at[1])

    lane8, lane16, lane128 = lanes((8, 128)), lanes((16, 128)), lanes((128, 128))
    sub8 = rows((8, 128))
    y_at = lax.rem(rows((128, 128)), 16)

    def comp_of(ref, c):
        return ref[c * 128 : (c + 1) * 128, :]

    def plane(ref, c, j):
        return ref[pl.ds(c * 128 + j, 8, stride=16), :]

    def put_plane(ref, c, j, value):
        ref[pl.ds(c * 128 + j, 8, stride=16), :] = value

    def z_pack(tiles, column, lane):
        packed = jnp.zeros(lane.shape, F32)
        for place, tile in enumerate(tiles):
            packed = jnp.where(lane == place, pltpu.roll(tile, (place - column) % 128, 1), packed)
        return packed

    def z_tiles(ref):
        return [ref[t * 16 : (t + 1) * 16, :] for t in range(24)]

    def x_stage(ref, stage):
        for c in range(3):
            xs[stage, 0, c] = ref[c * 128 + 112 : c * 128 + 128, :]
            xs[stage, 1, c] = ref[c * 128 : c * 128 + 16, :]

    def z_stage(ref, staging):
        tiles = z_tiles(ref)
        staging[0] = z_pack(tiles, 127, lane16)
        staging[1] = z_pack(tiles, 0, lane16)

    def spread(packed, c, lane_at):
        return jnp.concatenate(
            [pltpu.roll(packed, (lane_at - (c * 8 + x)) % 128, 1) for x in range(8)], axis=0
        )

    def around(u, x_low, x_high, z_low, z_high, cut=0):
        total = jnp.concatenate([x_low, u[:112]], axis=0) + jnp.concatenate([u[16:], x_high], axis=0)
        total = total + jnp.where(lane128 == 0, z_low, pltpu.roll(u, 1, 1))
        total = total + jnp.where(lane128 == 127, z_high, pltpu.roll(u, 127, 1))
        total = total + jnp.where(y_at <= cut, 0.0, pltpu.roll(u, 1, 0))
        return total + jnp.where(y_at >= 15 - cut, 0.0, pltpu.roll(u, 127, 0))

    def edges(k, x_got, z_low, z_high):
        value = jnp.where(sub8 == 0, x_got[0, k : k + 1, :], 0.0)
        value = value + jnp.where(sub8 == 7, x_got[1, k : k + 1, :], 0.0)
        value = value + jnp.where(lane8 == 0, pltpu.roll(z_low, (-k) % 128, 1), 0.0)
        return value + jnp.where(lane8 == 127, pltpu.roll(z_high, 127 - k, 1), 0.0)

    def beside(p, k, x_got, z_low, z_high):
        near = jnp.where(sub8 == 0, 0.0, pltpu.roll(p, 1, 0)) + jnp.where(sub8 == 7, 0.0, pltpu.roll(p, 7, 0))
        near = near + jnp.where(lane8 == 0, 0.0, pltpu.roll(p, 1, 1))
        near = near + jnp.where(lane8 == 127, 0.0, pltpu.roll(p, 127, 1))
        return near + edges(k, x_got, z_low, z_high)

    faces = ((0, (15, 14, 13)), (1, (0, 1, 2)))
    mine = ((0, (0, 1, 2)), (1, (15, 14, 13)))

    halves = jnp.where(lax.shift_right_logical(rows((128, 128)), 1) == lane128, 0.125, 0.0)

    def tile_of(ref, t):
        return ref[t * 8 : t * 8 + 8, :]

    def stage_rows(own, staging, at, n):
        for c in range(n):
            a, b, d, e = (tile_of(own, c * 4 + i) for i in range(4))
            up0, up1 = (jnp.where(sub8 < 4, pltpu.roll(v, 4, 0), w) for v, w in ((a, b), (d, e)))
            dn0, dn1 = (jnp.where(sub8 < 4, v, pltpu.roll(w, 4, 0)) for v, w in ((a, b), (d, e)))
            staging[0, at + c] = jnp.where(lane8 < 64, up0, pltpu.roll(up1, 64, 1))
            staging[1, at + c] = jnp.where(lane8 < 64, dn0, pltpu.roll(dn1, 64, 1))

    def unstage_rows(got, at, tile, n):
        for c in range(n):
            for i in range(4):
                low, high = got[0, at + c], got[1, at + c]
                if i >= 2:
                    low, high = pltpu.roll(low, 64, 1), pltpu.roll(high, 64, 1)
                if i % 2 == 0:
                    value = jnp.where(sub8 < 4, high, pltpu.roll(low, 4, 0))
                else:
                    value = jnp.where(sub8 < 4, pltpu.roll(high, 4, 0), low)
                tile[(c * 4 + i) * 8 : (c * 4 + i + 1) * 8, :] = value

    def join(own, tile, pack, staging, n):
        lane = lanes((n * 32, 128))
        pack[...] = jnp.where(lane < 64, own[...], pltpu.roll(tile[...], 64, 1))
        group = lane8 // 4
        sides = [jnp.zeros((8, 128), F32), jnp.zeros((8, 128), F32)]
        for t in range(8 * n):
            value = tile_of(own, t) if t < 4 * n else tile_of(tile, t - 4 * n)
            for side, column in ((0, 60), (1, 0)):
                sides[side] = jnp.where(group == t, pltpu.roll(value, (4 * t - column) % 128, 1), sides[side])
        staging[0], staging[1] = sides

    def assemble(pack, z_got, x_got, xz_got, c, n):
        tiles_ = []
        for place in range(12):
            t = c * 4 + place % 4
            if 4 <= place < 8:
                value, low, high = tile_of(pack, t), z_got[0], z_got[1]
            else:
                side = 0 if place < 4 else 1
                value, low, high = x_got[side, t * 8 : t * 8 + 8, :], xz_got[side, 0], xz_got[side, 1]
            for part, at in ((value, t), (pltpu.roll(value, 64, 1), 4 * n + t)):
                edge = jnp.where(
                    lane8 < 68, pltpu.roll(high, (64 - 4 * at) % 128, 1),
                    jnp.where(lane8 >= 124, pltpu.roll(low, (124 - 4 * at) % 128, 1), 0.0),
                )
                tiles_.append(jnp.where(lane8 < 64, part, edge))
        return jnp.concatenate(tiles_, axis=0)

    def take_turn(turn):
        for way, token in ((1, token_up), (-1, token_down)):
            for n in range(levels):
                if TURNS[n] == turn:

                    @pl.when(level == (n if way == 1 else levels - 1 - n))
                    def _(n=n, way=way, token=token):
                        if n > 0:
                            pl.semaphore_wait(token, 1)
                        if n < levels - 1:
                            pl.semaphore_signal(
                                token, inc=1, device_id={"gx": gx + way * ROW}, device_id_type=MESH
                            )

    fetches[0].wait()
    x_stage(vp, 0)
    z_stage(vp, zs1)
    fetches[1].wait()
    reaction = r[...]
    c_ref[...] = damping / (6.0 + reaction)
    halved = reaction.reshape(4, 2, 16, 128)
    tp[0:64, :] = (halved[:, 0] + halved[:, 1]).reshape(64, 128)
    mean_r = dot(tp[pl.ds(0, 32, stride=2), :] + tp[pl.ds(1, 32, stride=2), :], halves)
    inverse = damping / ((6.0 + 4.0 * mean_r) * 0.25)
    down[...] = inverse
    stage_rows(down, y1s, 5, 1)
    fetches[2].wait()
    for slot, (j, k, _) in faces:
        for c in range(3):
            y1s[slot, c] = plane(vp, c, j)
        y1s[slot, 3] = c_ref[pl.ds(j, 8, stride=16), :]
        y1s[slot, 4] = c_ref[pl.ds(k, 8, stride=16), :]
    fetches[3].wait()

    greeted = ROW - 1
    for test in (
        lower("gy"), upper("agg"), lower("agg"), crossing_up, crossing_down, level < levels - 1, level > 0
    ):
        greeted = greeted + test.astype(jnp.int32)
    pl.semaphore_wait(barrier, greeted)

    @pl.when(lower("gy"))
    def _():
        pl.semaphore_signal(ready, inc=1, device_id={"gy": here["gy"] - 1}, device_id_type=MESH)

    start(X1, "gx", both(xs.at[0]), xr1)
    start(Z1, "agg", both(zs1), zr1)
    start(Y1, "gy", both(y1s), y1r, (1,))

    first = []
    for c in range(3):
        pairs = comp_of(vp, c).reshape(4, 2, 16, 128)
        first.append(((pairs[:, 0] + pairs[:, 1]) * root_half).reshape(64, 128))
    a1 = jnp.concatenate(first, axis=0)
    even = lax.rem(rows((192, 128)), 2) == 0
    a1 = jnp.where(even, a1 + pltpu.roll(a1, 191, 0), pltpu.roll(a1, 1, 0) - a1) * root_half
    out_z, in_z = rows((128, 128)), lane128
    same = lax.shift_right_logical(out_z, 1) == lax.shift_right_logical(in_z, 1)
    minus = jnp.logical_and(lax.rem(out_z, 2) == 1, lax.rem(in_z, 2) == 1)
    pass_z = jnp.where(same, jnp.where(minus, -root_half, root_half), 0.0).astype(F32)
    turned = jnp.concatenate([dot(pass_z, a1, ((1,), (1,))), jnp.zeros((128, 64), F32)], axis=1)
    for t in range(n_gx):
        sendt[t] = turned[t * per : (t + 1) * per, :]

    arrive(X1, "gx", both(xs.at[0]), xr1)
    arrive(Z1, "agg", both(zs1), zr1)
    take_turn(1)
    z_low, z_high = zr1[0], zr1[1]
    for c in range(3):
        u = comp_of(vp, c)
        total = comp_of(f, c) + around(
            u, xr1[0, c], xr1[1, c], spread(z_low, c, 0), spread(z_high, c, 127)
        )
        gb[c * 128 : (c + 1) * 128, :] = total
        u1[c * 128 : (c + 1) * 128, :] = keep * u + c_ref[...] * total
    x_stage(u1, 1)
    start(X2, "gx", both(xs.at[1]), xr2)
    z_stage(u1, zs2)
    start(Z2, "agg", both(zs2), zr2)
    for slot, (j, k, _) in faces:
        for c in range(3):
            y2s[slot, c] = plane(gb, c, j)
            y2s[slot, 3 + c] = plane(f, c, j) + plane(u1, c, k)
    start(Y2, "gy", both(y2s), y2r, (1,))

    arrive(X2, "gx", both(xs.at[1]), xr2)
    arrive(Z2, "agg", both(zs2), zr2)
    take_turn(2)
    z_low, z_high = zr2[0], zr2[1]
    inner = jnp.logical_and(y_at >= 2, y_at <= 13)
    for c in range(3):
        u = comp_of(u1, c)
        total = comp_of(f, c) + around(
            u, xr2[0, c], xr2[1, c], spread(z_low, c, 0), spread(z_high, c, 127), 1
        )
        value = keep * u + c_ref[...] * total
        u2[c * 128 : (c + 1) * 128, :] = value
        uz[c * 128 : (c + 1) * 128, :] = jnp.where(inner, value, 0.0)
    x_stage(uz, 2)
    start(X3, "gx", both(xs.at[2]), xr3)
    z_stage(uz, zs3)
    start(Z3, "agg", both(zs3), zr3)
    for slot, (_, k, _) in faces:
        for c in range(3):
            y3s[slot, c] = plane(u2, c, k)
    start(Y3, "gy", both(y3s), y3r, (1,))

    arrive(X3, "gx", both(xs.at[2]), xr3)
    arrive(Z3, "agg", both(zs3), zr3)
    take_turn(3)
    z3_low, z3_high = zr3[0], zr3[1]
    for c in range(3):
        u = comp_of(uz, c)
        res = (
            comp_of(f, c) - (6.0 + r[...]) * u
            + around(u, xr3[0, c], xr3[1, c], spread(z3_low, c, 0), spread(z3_high, c, 127))
        )
        halved = res.reshape(4, 2, 16, 128)
        tp[c * 64 : (c + 1) * 64, :] = (
            (halved[:, 0] + halved[:, 1]).reshape(64, 128)
        )
    bown[...] = dot(tp[pl.ds(0, 96, stride=2), :] + tp[pl.ds(1, 96, stride=2), :], halves)
    stage_rows(bown, y4s, 0, 3)
    start(Y4, "gy", both(y4s), y4r, (1,))

    @pl.when(upper("gy"))
    def _():
        pl.semaphore_wait(ready, 1)

    for message, src, dst in ((Y1, y1s, y1r), (Y2, y2s, y2r), (Y3, y3s, y3r), (Y4, y4s, y4r)):
        start(message, "gy", both(src), dst, (0,))

    take_turn(4)

    arrive(Y1, "gy", both(y1s), y1r)
    unstage_rows(y1r, 5, dtile, 1)
    join(down, dtile, dpack, dzs, 1)
    start(DZ, "agg", both(dzs), dzr)
    start(DX, "gx", (dpack, dpack), dxr)

    arrive(Y2, "gy", both(y2s), y2r)
    for side, (j, _, _) in mine:
        c0, ch0 = c_ref[pl.ds(j, 8, stride=16), :], y1r[side, 3]
        for c in range(3):
            k = side * 3 + c
            vh = y1r[side, c]
            p1[k * 8 : k * 8 + 8, :] = plane(u1, c, j) + c0 * vh
            p1[48 + k * 8 : 56 + k * 8, :] = keep * vh + ch0 * (y2r[side, c] + plane(vp, c, j))
    xf2s[0, 0:12, :] = p1[pl.ds(7, 12, stride=8), :]
    xf2s[1, 0:12, :] = p1[pl.ds(0, 12, stride=8), :]
    start(XF2, "gx", both(xf2s), xf2r)
    tiles = [p1[k * 8 : k * 8 + 8, :] for k in range(12)]
    zf2s[0] = z_pack(tiles, 127, lane8)
    zf2s[1] = z_pack(tiles, 0, lane8)
    start(ZF2, "agg", both(zf2s), zf2r)

    take_turn(5)

    def send_line(step, carry):
        target = lax.rem(gx + step, n_gx)
        pltpu.make_async_remote_copy(
            src_ref=sendt.at[target], dst_ref=recvt.at[gx],
            send_sem=assem, recv_sem=arsem, device_id={"gx": target}, device_id_type=MESH,
        ).start()
        return carry

    lax.fori_loop(1, n_gx, send_line, 0)

    arrive(Y3, "gy", both(y3s), y3r)
    arrive(XF2, "gx", both(xf2s), xf2r)
    arrive(ZF2, "agg", both(zf2s), zf2r)
    f2_low, f2_high = zf2r[0], zf2r[1]
    for side, (j, j1, _) in mine:
        c0, c1 = c_ref[pl.ds(j, 8, stride=16), :], c_ref[pl.ds(j1, 8, stride=16), :]
        ch0, ch1 = y1r[side, 3], y1r[side, 4]
        for c in range(3):
            k = side * 3 + c
            own, halo = p1[k * 8 : k * 8 + 8, :], p1[48 + k * 8 : 56 + k * 8, :]
            near = beside(own, k, xf2r, f2_low, f2_high)
            p2[k * 8 : k * 8 + 8, :] = keep * own + c0 * (plane(f, c, j) + near + plane(u1, c, j1) + halo)
            p2[48 + k * 8 : 56 + k * 8, :] = plane(u2, c, j1) + c1 * own
            near = beside(halo, 6 + k, xf2r, f2_low, f2_high)
            p2[96 + k * 8 : 104 + k * 8, :] = keep * halo + ch0 * (
                y2r[side, 3 + c] + near + own
            )
            p2[144 + k * 8 : 152 + k * 8, :] = y3r[side, c] + ch1 * halo
    xf3s[0] = p2[pl.ds(7, 24, stride=8), :]
    xf3s[1] = p2[pl.ds(0, 24, stride=8), :]
    start(XF3, "gx", both(xf3s), xf3r)
    tiles = [p2[k * 8 : k * 8 + 8, :] for k in range(24)]
    zf3s[0] = z_pack(tiles, 127, lane8)
    zf3s[1] = z_pack(tiles, 0, lane8)
    start(ZF3, "agg", both(zf3s), zf3r)

    arrive(DZ, "agg", both(dzs), dzr)
    start(DXZ, "gx", (dzr, dzr), dxz)

    arrive(Y4, "gy", both(y4s), y4r)
    unstage_rows(y4r, 0, btile, 3)
    arrive(XF3, "gx", both(xf3s), xf3r)
    arrive(ZF3, "agg", both(zf3s), zf3r)
    f3_low, f3_high = zf3r[0], zf3r[1]
    for side, (j, j1, _) in mine:
        d0 = 6.0 + r[pl.ds(j, 8, stride=16), :]
        d1 = 6.0 + r[pl.ds(j1, 8, stride=16), :]
        ch0, ch1 = y1r[side, 3], y1r[side, 4]
        dh0 = jnp.where(ch0 > 0.0, damping / jnp.where(ch0 > 0.0, ch0, 1.0), 0.0)
        dh1 = jnp.where(ch1 > 0.0, damping / jnp.where(ch1 > 0.0, ch1, 1.0), 0.0)
        for c in range(3):
            k = side * 3 + c
            own0, own1, halo0, halo1 = (p2[n * 48 + k * 8 : n * 48 + k * 8 + 8, :] for n in range(4))
            near = beside(own0, k, xf3r, f3_low, f3_high) + beside(own1, 6 + k, xf3r, f3_low, f3_high)
            ps[k * 8 : k * 8 + 8, :] = near + own1 + halo0 + own0 - d0 * own0 - d1 * own1
            ps[48 + k * 8 : 56 + k * 8, :] = own1
            near = beside(halo0, 12 + k, xf3r, f3_low, f3_high) + beside(halo1, 18 + k, xf3r, f3_low, f3_high)
            ps[96 + k * 8 : 104 + k * 8, :] = near + halo1 + own0 + halo0 - dh0 * halo0 - dh1 * halo1
            ps[144 + k * 8 : 152 + k * 8, :] = halo1
            put_plane(u2, c, j, own0)
            put_plane(u2, c, j1, own1)
    line = dot(ps[pl.ds(0, 96, stride=2), :] + ps[pl.ds(1, 96, stride=2), :], halves)
    for side in (0, 1):
        at0, at1 = ((0, 1), (7, 6))[side]
        to0, to1 = ((7, 6), (0, 1))[side]
        for c in range(3):
            k = (side * 3 + c) * 4
            for ref, row0, row1, base in ((bown, at0, at1, 0), (btile, to0, to1, 48)):
                for row, part in ((row0, k), (row1, 24 + k)):
                    at = pl.ds(c * 32 + row, 4, stride=8)
                    ref[at, :] = ref[at, :] + line[base + part : base + part + 4]
    join(bown, btile, bpack, bzs, 3)
    start(BZ, "agg", both(bzs), bzr)
    start(BX, "gx", (bpack, bpack), bxr)

    arrive(DX, "gx", (dpack, dpack), dxr)
    arrive(DXZ, "gx", (dzr, dzr), dxz)
    cdext[...] = assemble(dpack, dzr, dxr, dxz, 0, 1)

    arrive(BZ, "agg", both(bzs), bzr)
    start(BXZ, "gx", (bzr, bzr), bxz)

    many = n_gx - 1
    lines = pltpu.make_async_remote_copy(
        src_ref=sendt.at[pl.ds(0, many)], dst_ref=recvt.at[pl.ds(0, many)],
        send_sem=assem, recv_sem=arsem, device_id={"gx": lax.rem(gx + 1, n_gx)}, device_id_type=MESH,
    )
    lines.wait_recv()
    lines.wait_send()
    recvt[gx] = sendt[gx]
    for k in range(per):
        got = recvt[:, k, :]
        wide = dot(got[:, 0:192], mcat[...], ((0,), (0,)))
        for c in range(3):
            value = 0.0
            for m in range(4):
                at = (c * 4 + m) * 16
                value = value + wide[at : at + 16, m * 4 * n_gx : (m + 1) * 4 * n_gx]
            comp[c, :, k, :] = value

    arrive(BX, "gx", (bpack, bpack), bxr)
    arrive(BXZ, "gx", (bzr, bzr), bxz)

    y16 = lax.rem(rows((192, 128)), 16)
    fine = lane128 // 2 == rows((128, 128))
    beyond = jnp.logical_or(
        jnp.logical_and(lane128 == 0, rows((128, 128)) == 127),
        jnp.logical_and(lane128 == 127, rows((128, 128)) == 64),
    )
    up = jnp.concatenate([jnp.where(fine, 1.0, 0.0), jnp.where(beyond, 1.0, 0.0)], axis=1).astype(F32)
    none = jnp.zeros((16, 128), F32)
    for c in range(3):
        rhs_c = assemble(bpack, bzr, bxr, bxz, c, 3)
        weight = cdext[...]
        e = weight * rhs_c
        for _ in range(COARSE_SWEEPS - 1):
            near = jnp.concatenate([none, e[:176]], axis=0) + jnp.concatenate([e[16:], none], axis=0)
            near = near + pltpu.roll(e, 1, 1) + pltpu.roll(e, 127, 1)
            near = near + jnp.where(y16 == 0, pltpu.roll(e, 192 - 15, 0), pltpu.roll(e, 1, 0))
            near = near + jnp.where(y16 == 15, pltpu.roll(e, 15, 0), pltpu.roll(e, 191, 0))
            e = keep * e + weight * (rhs_c + 0.25 * near)
        refined = dot(e[48:144], up)
        eu[c * 96 : (c + 1) * 96, :] = refined[:, 0:128]
        for ref, part in ((cf, refined[:, 0:128]), (cz, refined[:, 128:256])):
            main = part.reshape(6, 16, 128)[:, 0:8].reshape(48, 128)
            ref[pl.ds(c * 96, 48, stride=2), :] = main
            ref[pl.ds(c * 96 + 1, 48, stride=2), :] = main
        for side, row in ((0, 15), (1, 8)):
            line_ = eu[pl.ds(c * 96 + 16 + row, 4, stride=16), :]
            at = (side * 3 + c) * 8
            ph[pl.ds(at, 4, stride=2), :] = line_
            ph[pl.ds(at + 1, 4, stride=2), :] = line_

    def doubled(ref, c):
        value = ref[c * 96 + 16 : c * 96 + 80, :].reshape(4, 1, 16, 128)
        return jnp.broadcast_to(value, (4, 2, 16, 128)).reshape(128, 128)

    for c in range(3):
        w = comp_of(u2, c) + doubled(cf, c)
        outer = doubled(cz, c)
        total = comp_of(f, c) + around(
            w,
            xr3[0, c] + cf[c * 96 : c * 96 + 16, :],
            xr3[1, c] + cf[c * 96 + 80 : c * 96 + 96, :],
            spread(z3_low, c, 0) + outer,
            spread(z3_high, c, 127) + outer,
        )
        vel[c * 128 : (c + 1) * 128, :] = keep * w + c_ref[...] * total
    for side, (j, j1, _) in mine:
        c0, c1 = c_ref[pl.ds(j, 8, stride=16), :], c_ref[pl.ds(j1, 8, stride=16), :]
        for c in range(3):
            k = side * 3 + c
            more = edges(k, xf3r, f3_low, f3_high)
            more = more + p2[96 + k * 8 : 104 + k * 8, :] + ph[k * 8 : k * 8 + 8, :]
            put_plane(vel, c, j, plane(vel, c, j) + c0 * more)
            more = edges(6 + k, xf3r, f3_low, f3_high)
            put_plane(vel, c, j1, plane(vel, c, j1) + c1 * more)

    for message, axis, src, dst, side in ends:

        @pl.when(upper(axis) if side == 0 else lower(axis))
        def _(args=(message, axis, src, dst, side)):
            one_copy(*args).wait_send()


def on_device(sizes, velocity_prev, forcing, reaction):
    n_agg, n_gx, n_gy = sizes
    per = 128 // n_gx

    def v(*shape):
        return pltpu.VMEM(shape, F32)

    scratch = [
        v(384, 128), v(384, 128), v(128, 128), v(n_gx, 16 * n_gx),
        v(128, 128), v(384, 128), v(384, 128), v(384, 128), v(384, 128), v(192, 128),
        v(n_gx, per, 256), v(n_gx, per, 256),
        v(3, 2, 3, 16, 128), v(2, 3, 16, 128), v(2, 3, 16, 128), v(2, 3, 16, 128),
    ]
    scratch += [v(2, 16, 128)] * 6
    scratch += [v(96, 128), v(192, 128), v(192, 128)]
    scratch += [v(2, 16, 128)] * 2 + [v(2, 8, 128)] * 2 + [v(2, 24, 128)] * 2 + [v(2, 8, 128)] * 2
    scratch += [v(2, 6, 8, 128)] * 4 + [v(2, 3, 8, 128)] * 4
    for n in (1, 3):
        scratch += [v(n * 32, 128)] * 3 + [v(2, n * 32, 128), v(2, 8, 128), v(2, 8, 128), v(2, 2, 8, 128)]
    scratch += [v(192, 128), v(288, 128), v(288, 128), v(288, 128), v(48, 128)]
    dma = pltpu.SemaphoreType.DMA
    scratch += [dma((4,)), dma((COUNT, 2)), dma((COUNT, 2)), dma, dma]
    scratch += [pltpu.SemaphoreType.REGULAR] * 3
    vmem = pl.BlockSpec(memory_space=pltpu.VMEM)
    velocity, compressed = pl.pallas_call(
        functools.partial(kernel, sizes),
        out_shape=(
            jax.ShapeDtypeStruct((384, 128), F32),
            jax.ShapeDtypeStruct((3, 16, per, 4 * n_gx), F32),
        ),
        in_specs=[pl.BlockSpec(memory_space=pltpu.HBM)] * 4,
        out_specs=(vmem, vmem),
        scratch_shapes=scratch,
        compiler_params=pltpu.CompilerParams(collective_id=0, has_side_effects=True),
        name="vcycle",
    )(
        velocity_prev.reshape(384, 128), forcing.reshape(384, 128), reaction.reshape(128, 128),
        jnp.asarray(haar_matrix(n_gx)),
    )
    return velocity.reshape(3, 8, 16, 128), compressed


def solution(mesh):
    placed = (P(None, "gx", "gy", "agg"), P(None, "gx", "gy", "agg"), P("gx", "gy", "agg"))
    sizes = tuple(mesh.shape[name] for name in ("agg", "gx", "gy"))
    return jax.shard_map(
        functools.partial(on_device, sizes),
        mesh=mesh,
        in_specs=placed,
        out_specs=(P(None, "gx", "gy", "agg"), P(None, "gy", ("agg", "gx"), None)),
        check_vma=False,
    )
```

time: 267 us -> 59.6 us (0.22)
  the two profiles are of different devices: /device:TPU:232 before, /device:TPU:897 now
where the time goes in v2:
time: 59.6 us; the launch traced here: 59.4 us
  Pallas kernels  56.5 us (95%)
  local copies, waits for them, and re-layouts  2.29 us (4%)
  between operations  0.65 us (1%)
    pallas_call x1, Pallas kernels, on_device(): pl.pallas_call(functools.partial(kernel, sizes), out_shape=(jax.ShapeDtyp...  56.5 us
    unnamed x4, local copies, waits for them, and re-layouts  2.29 us

profile of v2, /device:TPU:897, one launch (start us, length us, event | category | flops | bytes accessed | tf_op | source)
XLA Modules:
  0.0 59.4 jit_solution(17411404097198739027)
XLA Ops:
  0.6 56.5 %vcycle.1 = (f32[384,128]{1,0:T(8,128)}, f32[3,16,4,128]{3,2,1,0:T(4,128)}) custom-call(f32[384,128]{1,0:T(8,128)} %bitcast.5, f32[384,128]{1,0:T(8,128)} %bitcast.6, f32[128,128]{1,0:T(8,128)} %bitcast.7, f32[32,512]{1,0:T(8,128)} %constant.2.clone.m_in), custom_call_target="tpu_custom_call" | custom-call | tf_op jit(solution)/shard_map/vcycle/pallas_call | solution.py:596
  57.1 0.0 copy-start
  57.1 1.6 %copy.8 = f32[3,8,16,128]{3,2,1,0:T(8,128)} copy(f32[3,8,16,128]{3,2,1,0:T(8,128)} %bitcast.4) | data formatting | bytes 393216
  58.8 0.0 copy-done
  58.8 0.6 %copy.9 = f32[3,16,4,128]{3,2,1,0:T(4,128)} copy(f32[3,16,4,128]{3,2,1,0:T(4,128)S(1)} %copy-done) | data formatting | bytes 196608
Async XLA Ops:
  57.1 1.7 %copy-start = (f32[3,16,4,128]{3,2,1,0:T(4,128)S(1)}, f32[3,16,4,128]{3,2,1,0:T(4,128)}, u32[]{:S(2)}) copy-start(f32[3,16,4,128]{3,2,1,0:T(4,128)} %get-tuple-element.9) | copy-start | bytes 294916

commit v3 on v2

--- a/solution.py
+++ b/solution.py
@@ -262,7 +262,21 @@
 
     fetches[0].wait()
     x_stage(vp, 0)
+    greeted = ROW - 1
+    for test in (
+        lower("gy"), upper("agg"), lower("agg"), crossing_up, crossing_down, level < levels - 1, level > 0
+    ):
+        greeted = greeted + test.astype(jnp.int32)
+    pl.semaphore_wait(barrier, greeted)
+
+    @pl.when(lower("gy"))
+    def _():
+        pl.semaphore_signal(ready, inc=1, device_id={"gy": here["gy"] - 1}, device_id_type=MESH)
+
+    start(X1, "gx", both(xs.at[0]), xr1)
     z_stage(vp, zs1)
+    start(Z1, "agg", both(zs1), zr1)
+
     fetches[1].wait()
     reaction = r[...]
     c_ref[...] = damping / (6.0 + reaction)
@@ -272,28 +286,14 @@
     inverse = damping / ((6.0 + 4.0 * mean_r) * 0.25)
     down[...] = inverse
     stage_rows(down, y1s, 5, 1)
-    fetches[2].wait()
     for slot, (j, k, _) in faces:
         for c in range(3):
             y1s[slot, c] = plane(vp, c, j)
         y1s[slot, 3] = c_ref[pl.ds(j, 8, stride=16), :]
         y1s[slot, 4] = c_ref[pl.ds(k, 8, stride=16), :]
+    start(Y1, "gy", both(y1s), y1r, (1,))
+    fetches[2].wait()
     fetches[3].wait()
-
-    greeted = ROW - 1
-    for test in (
-        lower("gy"), upper("agg"), lower("agg"), crossing_up, crossing_down, level < levels - 1, level > 0
-    ):
-        greeted = greeted + test.astype(jnp.int32)
-    pl.semaphore_wait(barrier, greeted)
-
-    @pl.when(lower("gy"))
-    def _():
-        pl.semaphore_signal(ready, inc=1, device_id={"gy": here["gy"] - 1}, device_id_type=MESH)
-
-    start(X1, "gx", both(xs.at[0]), xr1)
-    start(Z1, "agg", both(zs1), zr1)
-    start(Y1, "gy", both(y1s), y1r, (1,))
 
     first = []
     for c in range(3):
@@ -353,6 +353,13 @@
             y3s[slot, c] = plane(u2, c, k)
     start(Y3, "gy", both(y3s), y3r, (1,))
 
+    @pl.when(upper("gy"))
+    def _():
+        pl.semaphore_wait(ready, 1)
+
+    for message, src, dst in ((Y1, y1s, y1r), (Y2, y2s, y2r), (Y3, y3s, y3r)):
+        start(message, "gy", both(src), dst, (0,))
+
     arrive(X3, "gx", both(xs.at[2]), xr3)
     arrive(Z3, "agg", both(zs3), zr3)
     take_turn(3)
@@ -369,14 +376,7 @@
         )
     bown[...] = dot(tp[pl.ds(0, 96, stride=2), :] + tp[pl.ds(1, 96, stride=2), :], halves)
     stage_rows(bown, y4s, 0, 3)
-    start(Y4, "gy", both(y4s), y4r, (1,))
-
-    @pl.when(upper("gy"))
-    def _():
-        pl.semaphore_wait(ready, 1)
-
-    for message, src, dst in ((Y1, y1s, y1r), (Y2, y2s, y2r), (Y3, y3s, y3r), (Y4, y4s, y4r)):
-        start(message, "gy", both(src), dst, (0,))
+    start(Y4, "gy", both(y4s), y4r)
 
     take_turn(4)
 
@@ -569,6 +569,17 @@
             one_copy(*args).wait_send()
 
 
+def put_kernel(velocity, compressed, velocity_out, compressed_out, sem):
+    copies = [
+        pltpu.make_async_copy(velocity, velocity_out, sem.at[0]),
+        pltpu.make_async_copy(compressed, compressed_out, sem.at[1]),
+    ]
+    for copy in copies:
+        copy.start()
+    for copy in copies:
+        copy.wait()
+
+
 def on_device(sizes, velocity_prev, forcing, reaction):
     n_agg, n_gx, n_gy = sizes
     per = 128 // n_gx
@@ -602,12 +613,28 @@
         in_specs=[pl.BlockSpec(memory_space=pltpu.HBM)] * 4,
         out_specs=(vmem, vmem),
         scratch_shapes=scratch,
-        compiler_params=pltpu.CompilerParams(collective_id=0, has_side_effects=True),
+        compiler_params=pltpu.CompilerParams(
+            collective_id=0, has_side_effects=True, vmem_limit_bytes=12 * 2**20
+        ),
         name="vcycle",
     )(
-        velocity_prev.reshape(384, 128), forcing.reshape(384, 128), reaction.reshape(128, 128),
-        jnp.asarray(haar_matrix(n_gx)),
+        *(
+            pltpu.with_memory_space_constraint(value, pltpu.HBM)
+            for value in (
+                velocity_prev.reshape(384, 128), forcing.reshape(384, 128), reaction.reshape(128, 128),
+                jnp.asarray(haar_matrix(n_gx)),
+            )
+        )
     )
+    velocity, compressed = pl.pallas_call(
+        put_kernel,
+        out_shape=tuple(jax.ShapeDtypeStruct(value.shape, F32) for value in (velocity, compressed)),
+        in_specs=[vmem] * 2,
+        out_specs=[pl.BlockSpec(memory_space=pltpu.HBM)] * 2,
+        scratch_shapes=[dma((2,))],
+        compiler_params=pltpu.CompilerParams(vmem_limit_bytes=12 * 2**20),
+        name="put",
+    )(velocity, compressed)
     return velocity.reshape(3, 8, 16, 128), compressed
 
 

time: 59.6 us -> 53.3 us (0.89)
  Pallas kernels: 56.5 us -> 52.4 us
  local copies, waits for them, and re-layouts: 2.29 us -> 0 us
    pallas_call x1, Pallas kernels: 56.5 us -> 51.6 us  [on_device(): pl.pallas_call(functools.partial(kernel, sizes), out_shape=(jax.ShapeDtyp...]
    unnamed x4 -> x0, local copies, waits for them, and re-layouts: 2.29 us -> none
    pallas_call x0 -> x1, Pallas kernels: none -> 0.72 us  [on_device(): pl.pallas_call(put_kernel, out_shape=tuple((jax.ShapeDtypeStruct(value.sh...]
where the time goes in v3:
time: 53.3 us; the launch traced here: 53 us
  Pallas kernels  52.4 us (98%)
  between operations  0.64 us (1%)
    pallas_call x1, Pallas kernels, on_device(): pl.pallas_call(functools.partial(kernel, sizes), out_shape=(jax.ShapeDtyp...  51.6 us

profile of v3, /device:TPU:897, one launch (start us, length us, event | category | flops | bytes accessed | tf_op | source)
XLA Modules:
  0.0 53.0 jit_solution(1345327805039468308)
XLA Ops:
  0.6 51.6 %vcycle.1 = (f32[384,128]{1,0:T(8,128)S(1)}, f32[3,16,4,128]{3,2,1,0:T(4,128)S(1)}) custom-call(f32[384,128]{1,0:T(8,128)} %bitcast.4, f32[384,128]{1,0:T(8,128)} %bitcast.5, f32[128,128]{1,0:T(8,128)} %bitcast.6, f32[32,512]{1,0:T(8,128)} %constant.2.clone.m_in), custom_call_target="tpu_custom_call" | custom-call | tf_op jit(solution)/shard_map/vcycle/pallas_call | solution.py:607
  52.3 0.7 %put.1 = (f32[384,128]{1,0:T(8,128)}, f32[3,16,4,128]{3,2,1,0:T(4,128)}) custom-call(f32[384,128]{1,0:T(8,128)S(1)} %get-tuple-element.6.velocity, f32[3,16,4,128]{3,2,1,0:T(4,128)S(1)} %get-tuple-element.7.compressed), custom_call_target="tpu_custom_call" | custom-call | tf_op jit(solution)/shard_map/put/pallas_call | solution.py:629

commit v4 on v3

--- a/solution.py
+++ b/solution.py
@@ -50,9 +50,9 @@
 
 def kernel(
     sizes, vp_in, f_in, r_in, m_in, vel, comp,
-    vp, f, r, mcat, c_ref, u1, u2, uz, gb, tp, sendt, recvt,
+    vp, f, r, mcat, c_ref, u1, u2, tp, sendt, recvt,
     xs, xr1, xr2, xr3, zs1, zr1, zs2, zr2, zs3, zr3,
-    p1, p2, ps, xf2s, xf2r, zf2s, zf2r, xf3s, xf3r, zf3s, zf3r,
+    p1, p2, po, ps, xf2s, xf2r, zf2s, zf2r, xf3s, xf3r, zf3s, zf3r,
     y1s, y1r, y2s, y2r, y3s, y3r, y4s, y4r,
     down, dtile, dpack, dxr, dzs, dzr, dxz, bown, btile, bpack, bxr, bzs, bzr, bxz,
     cdext, cf, cz, eu, ph,
@@ -86,7 +86,12 @@
 
     crossing_up = jnp.logical_and(place_x == ROW - 1, upper("gx"))
     crossing_down = jnp.logical_and(place_x == 0, lower("gx"))
-    greet(upper("gy"), {"gy": here["gy"] + 1})
+    last_pair = n_gy - 2
+    gy = here["gy"]
+    sure = ((gy == last_pair), jnp.logical_and(gy > 0, gy <= last_pair))
+    later = ((gy < last_pair), (gy > last_pair))
+    greet(gy < last_pair, {"gy": gy + 1})
+    greet(gy > last_pair, {"gy": gy - 1})
     greet(upper("agg"), {"agg": here["agg"] + 1})
     greet(lower("agg"), {"agg": here["agg"] - 1})
     for step in range(1, ROW):
@@ -115,6 +120,13 @@
 
     ends = []
 
+    def send_y(message, src, dst, tests):
+        for side, test in enumerate(tests):
+
+            @pl.when(test)
+            def _(side=side):
+                one_copy(message, "gy", both(src), dst, side).start()
+
     def start(message, axis, src, dst, sides=(0, 1)):
         for side in sides:
 
@@ -171,12 +183,12 @@
             [pltpu.roll(packed, (lane_at - (c * 8 + x)) % 128, 1) for x in range(8)], axis=0
         )
 
-    def around(u, x_low, x_high, z_low, z_high, cut=0):
+    def around(u, x_low, x_high, z_low, z_high):
         total = jnp.concatenate([x_low, u[:112]], axis=0) + jnp.concatenate([u[16:], x_high], axis=0)
         total = total + jnp.where(lane128 == 0, z_low, pltpu.roll(u, 1, 1))
         total = total + jnp.where(lane128 == 127, z_high, pltpu.roll(u, 127, 1))
-        total = total + jnp.where(y_at <= cut, 0.0, pltpu.roll(u, 1, 0))
-        return total + jnp.where(y_at >= 15 - cut, 0.0, pltpu.roll(u, 127, 0))
+        total = total + jnp.where(y_at == 0, 0.0, pltpu.roll(u, 1, 0))
+        return total + jnp.where(y_at == 15, 0.0, pltpu.roll(u, 127, 0))
 
     def edges(k, x_got, z_low, z_high):
         value = jnp.where(sub8 == 0, x_got[0, k : k + 1, :], 0.0)
@@ -190,8 +202,8 @@
         near = near + jnp.where(lane8 == 127, 0.0, pltpu.roll(p, 127, 1))
         return near + edges(k, x_got, z_low, z_high)
 
-    faces = ((0, (15, 14, 13)), (1, (0, 1, 2)))
-    mine = ((0, (0, 1, 2)), (1, (15, 14, 13)))
+    faces = ((0, (15, 14)), (1, (0, 1)))
+    mine = ((0, (0, 1)), (1, (15, 14)))
 
     halves = jnp.where(lax.shift_right_logical(rows((128, 128)), 1) == lane128, 0.125, 0.0)
 
@@ -264,14 +276,16 @@
     x_stage(vp, 0)
     greeted = ROW - 1
     for test in (
-        lower("gy"), upper("agg"), lower("agg"), crossing_up, crossing_down, level < levels - 1, level > 0
+        sure[0], sure[1], upper("agg"), lower("agg"), crossing_up, crossing_down, level < levels - 1, level > 0
     ):
         greeted = greeted + test.astype(jnp.int32)
     pl.semaphore_wait(barrier, greeted)
 
-    @pl.when(lower("gy"))
-    def _():
-        pl.semaphore_signal(ready, inc=1, device_id={"gy": here["gy"] - 1}, device_id_type=MESH)
+    for test, step in zip(sure, (1, -1)):
+
+        @pl.when(test)
+        def _(step=step):
+            pl.semaphore_signal(ready, inc=1, device_id={"gy": gy + step}, device_id_type=MESH)
 
     start(X1, "gx", both(xs.at[0]), xr1)
     z_stage(vp, zs1)
@@ -286,12 +300,12 @@
     inverse = damping / ((6.0 + 4.0 * mean_r) * 0.25)
     down[...] = inverse
     stage_rows(down, y1s, 5, 1)
-    for slot, (j, k, _) in faces:
+    for slot, (j, k) in faces:
         for c in range(3):
             y1s[slot, c] = plane(vp, c, j)
         y1s[slot, 3] = c_ref[pl.ds(j, 8, stride=16), :]
         y1s[slot, 4] = c_ref[pl.ds(k, 8, stride=16), :]
-    start(Y1, "gy", both(y1s), y1r, (1,))
+    send_y(Y1, y1s, y1r, sure)
     fetches[2].wait()
     fetches[3].wait()
 
@@ -312,60 +326,56 @@
 
     arrive(X1, "gx", both(xs.at[0]), xr1)
     arrive(Z1, "agg", both(zs1), zr1)
-    take_turn(1)
     z_low, z_high = zr1[0], zr1[1]
     for c in range(3):
         u = comp_of(vp, c)
         total = comp_of(f, c) + around(
             u, xr1[0, c], xr1[1, c], spread(z_low, c, 0), spread(z_high, c, 127)
         )
-        gb[c * 128 : (c + 1) * 128, :] = total
         u1[c * 128 : (c + 1) * 128, :] = keep * u + c_ref[...] * total
     x_stage(u1, 1)
     start(X2, "gx", both(xs.at[1]), xr2)
     z_stage(u1, zs2)
     start(Z2, "agg", both(zs2), zr2)
-    for slot, (j, k, _) in faces:
-        for c in range(3):
-            y2s[slot, c] = plane(gb, c, j)
-            y2s[slot, 3 + c] = plane(f, c, j) + plane(u1, c, k)
-    start(Y2, "gy", both(y2s), y2r, (1,))
+    for slot, (j, _) in faces:
+        for c in range(3):
+            y2s[slot, c] = plane(u1, c, j)
+    send_y(Y2, y2s, y2r, sure)
+    take_turn(1)
 
     arrive(X2, "gx", both(xs.at[1]), xr2)
     arrive(Z2, "agg", both(zs2), zr2)
-    take_turn(2)
     z_low, z_high = zr2[0], zr2[1]
-    inner = jnp.logical_and(y_at >= 2, y_at <= 13)
     for c in range(3):
         u = comp_of(u1, c)
         total = comp_of(f, c) + around(
-            u, xr2[0, c], xr2[1, c], spread(z_low, c, 0), spread(z_high, c, 127), 1
-        )
-        value = keep * u + c_ref[...] * total
-        u2[c * 128 : (c + 1) * 128, :] = value
-        uz[c * 128 : (c + 1) * 128, :] = jnp.where(inner, value, 0.0)
-    x_stage(uz, 2)
+            u, xr2[0, c], xr2[1, c], spread(z_low, c, 0), spread(z_high, c, 127)
+        )
+        u2[c * 128 : (c + 1) * 128, :] = keep * u + c_ref[...] * total
+    x_stage(u2, 2)
     start(X3, "gx", both(xs.at[2]), xr3)
-    z_stage(uz, zs3)
+    z_stage(u2, zs3)
     start(Z3, "agg", both(zs3), zr3)
-    for slot, (_, k, _) in faces:
-        for c in range(3):
-            y3s[slot, c] = plane(u2, c, k)
-    start(Y3, "gy", both(y3s), y3r, (1,))
-
-    @pl.when(upper("gy"))
+    for slot, (j, _) in faces:
+        for c in range(3):
+            y3s[slot, c] = plane(u2, c, j)
+    send_y(Y3, y3s, y3r, sure)
+
+    @pl.when(jnp.logical_or(later[0], later[1]))
     def _():
         pl.semaphore_wait(ready, 1)
 
     for message, src, dst in ((Y1, y1s, y1r), (Y2, y2s, y2r), (Y3, y3s, y3r)):
-        start(message, "gy", both(src), dst, (0,))
+        send_y(message, src, dst, later)
+        for side in (0, 1):
+            ends.append((message, "gy", both(src), dst, side))
+    take_turn(2)
 
     arrive(X3, "gx", both(xs.at[2]), xr3)
     arrive(Z3, "agg", both(zs3), zr3)
-    take_turn(3)
     z3_low, z3_high = zr3[0], zr3[1]
     for c in range(3):
-        u = comp_of(uz, c)
+        u = comp_of(u2, c)
         res = (
             comp_of(f, c) - (6.0 + r[...]) * u
             + around(u, xr3[0, c], xr3[1, c], spread(z3_low, c, 0), spread(z3_high, c, 127))
@@ -377,23 +387,21 @@
     bown[...] = dot(tp[pl.ds(0, 96, stride=2), :] + tp[pl.ds(1, 96, stride=2), :], halves)
     stage_rows(bown, y4s, 0, 3)
     start(Y4, "gy", both(y4s), y4r)
-
-    take_turn(4)
+    take_turn(3)
+
 
     arrive(Y1, "gy", both(y1s), y1r)
     unstage_rows(y1r, 5, dtile, 1)
     join(down, dtile, dpack, dzs, 1)
     start(DZ, "agg", both(dzs), dzr)
     start(DX, "gx", (dpack, dpack), dxr)
-
-    arrive(Y2, "gy", both(y2s), y2r)
-    for side, (j, _, _) in mine:
-        c0, ch0 = c_ref[pl.ds(j, 8, stride=16), :], y1r[side, 3]
+    take_turn(4)
+
+    for side, (j, _) in mine:
         for c in range(3):
             k = side * 3 + c
-            vh = y1r[side, c]
-            p1[k * 8 : k * 8 + 8, :] = plane(u1, c, j) + c0 * vh
-            p1[48 + k * 8 : 56 + k * 8, :] = keep * vh + ch0 * (y2r[side, c] + plane(vp, c, j))
+            p1[k * 8 : k * 8 + 8, :] = c_ref[pl.ds(j, 8, stride=16), :] * y1r[side, c]
+            p1[48 + k * 8 : 56 + k * 8, :] = y1r[side, 3] * plane(vp, c, j)
     xf2s[0, 0:12, :] = p1[pl.ds(7, 12, stride=8), :]
     xf2s[1, 0:12, :] = p1[pl.ds(0, 12, stride=8), :]
     start(XF2, "gx", both(xf2s), xf2r)
@@ -414,24 +422,23 @@
 
     lax.fori_loop(1, n_gx, send_line, 0)
 
-    arrive(Y3, "gy", both(y3s), y3r)
     arrive(XF2, "gx", both(xf2s), xf2r)
     arrive(ZF2, "agg", both(zf2s), zf2r)
+    arrive(Y2, "gy", both(y2s), y2r)
     f2_low, f2_high = zf2r[0], zf2r[1]
-    for side, (j, j1, _) in mine:
+    for side, (j, j1) in mine:
         c0, c1 = c_ref[pl.ds(j, 8, stride=16), :], c_ref[pl.ds(j1, 8, stride=16), :]
         ch0, ch1 = y1r[side, 3], y1r[side, 4]
         for c in range(3):
             k = side * 3 + c
             own, halo = p1[k * 8 : k * 8 + 8, :], p1[48 + k * 8 : 56 + k * 8, :]
-            near = beside(own, k, xf2r, f2_low, f2_high)
-            p2[k * 8 : k * 8 + 8, :] = keep * own + c0 * (plane(f, c, j) + near + plane(u1, c, j1) + halo)
-            p2[48 + k * 8 : 56 + k * 8, :] = plane(u2, c, j1) + c1 * own
-            near = beside(halo, 6 + k, xf2r, f2_low, f2_high)
-            p2[96 + k * 8 : 104 + k * 8, :] = keep * halo + ch0 * (
-                y2r[side, 3 + c] + near + own
-            )
-            p2[144 + k * 8 : 152 + k * 8, :] = y3r[side, c] + ch1 * halo
+            near = beside(own, k, xf2r, f2_low, f2_high) + y2r[side, c] + halo
+            p2[k * 8 : k * 8 + 8, :] = keep * own + c0 * near
+            p2[48 + k * 8 : 56 + k * 8, :] = c1 * own
+            near = beside(halo, 6 + k, xf2r, f2_low, f2_high) + plane(u1, c, j) + own
+            p2[96 + k * 8 : 104 + k * 8, :] = keep * halo + ch0 * near
+            p2[144 + k * 8 : 152 + k * 8, :] = ch1 * halo
+            po[k * 8 : k * 8 + 8, :] = damping * (keep * plane(vp, c, j) + near)
     xf3s[0] = p2[pl.ds(7, 24, stride=8), :]
     xf3s[1] = p2[pl.ds(0, 24, stride=8), :]
     start(XF3, "gx", both(xf3s), xf3r)
@@ -443,28 +450,32 @@
     arrive(DZ, "agg", both(dzs), dzr)
     start(DXZ, "gx", (dzr, dzr), dxz)
 
+    arrive(Y3, "gy", both(y3s), y3r)
     arrive(Y4, "gy", both(y4s), y4r)
     unstage_rows(y4r, 0, btile, 3)
     arrive(XF3, "gx", both(xf3s), xf3r)
     arrive(ZF3, "agg", both(zf3s), zf3r)
     f3_low, f3_high = zf3r[0], zf3r[1]
-    for side, (j, j1, _) in mine:
+    for side, (j, j1) in mine:
         d0 = 6.0 + r[pl.ds(j, 8, stride=16), :]
-        d1 = 6.0 + r[pl.ds(j1, 8, stride=16), :]
-        ch0, ch1 = y1r[side, 3], y1r[side, 4]
-        dh0 = jnp.where(ch0 > 0.0, damping / jnp.where(ch0 > 0.0, ch0, 1.0), 0.0)
-        dh1 = jnp.where(ch1 > 0.0, damping / jnp.where(ch1 > 0.0, ch1, 1.0), 0.0)
         for c in range(3):
             k = side * 3 + c
             own0, own1, halo0, halo1 = (p2[n * 48 + k * 8 : n * 48 + k * 8 + 8, :] for n in range(4))
+            whole0 = plane(u2, c, j) + own0
+            beyond0 = y3r[side, c] + halo0
             near = beside(own0, k, xf3r, f3_low, f3_high) + beside(own1, 6 + k, xf3r, f3_low, f3_high)
-            ps[k * 8 : k * 8 + 8, :] = near + own1 + halo0 + own0 - d0 * own0 - d1 * own1
+            ps[k * 8 : k * 8 + 8, :] = (
+                near + own1 + beyond0 + own0 - d0 * own0 - damping * p1[k * 8 : k * 8 + 8, :]
+            )
             ps[48 + k * 8 : 56 + k * 8, :] = own1
             near = beside(halo0, 12 + k, xf3r, f3_low, f3_high) + beside(halo1, 18 + k, xf3r, f3_low, f3_high)
-            ps[96 + k * 8 : 104 + k * 8, :] = near + halo1 + own0 + halo0 - dh0 * halo0 - dh1 * halo1
+            ps[96 + k * 8 : 104 + k * 8, :] = (
+                near + halo1 + whole0 + halo0 - po[k * 8 : k * 8 + 8, :] - damping * p1[48 + k * 8 : 56 + k * 8, :]
+            )
             ps[144 + k * 8 : 152 + k * 8, :] = halo1
-            put_plane(u2, c, j, own0)
-            put_plane(u2, c, j1, own1)
+            put_plane(u2, c, j, whole0)
+            put_plane(u2, c, j1, plane(u2, c, j1) + own1)
+            ph[k * 8 : k * 8 + 8, :] = beyond0
     line = dot(ps[pl.ds(0, 96, stride=2), :] + ps[pl.ds(1, 96, stride=2), :], halves)
     for side in (0, 1):
         at0, at1 = ((0, 1), (7, 6))[side]
@@ -534,8 +545,9 @@
         for side, row in ((0, 15), (1, 8)):
             line_ = eu[pl.ds(c * 96 + 16 + row, 4, stride=16), :]
             at = (side * 3 + c) * 8
-            ph[pl.ds(at, 4, stride=2), :] = line_
-            ph[pl.ds(at + 1, 4, stride=2), :] = line_
+            for step in (0, 1):
+                spot = pl.ds(at + step, 4, stride=2)
+                ph[spot, :] = ph[spot, :] + line_
 
     def doubled(ref, c):
         value = ref[c * 96 + 16 : c * 96 + 80, :].reshape(4, 1, 16, 128)
@@ -552,12 +564,12 @@
             spread(z3_high, c, 127) + outer,
         )
         vel[c * 128 : (c + 1) * 128, :] = keep * w + c_ref[...] * total
-    for side, (j, j1, _) in mine:
+    for side, (j, j1) in mine:
         c0, c1 = c_ref[pl.ds(j, 8, stride=16), :], c_ref[pl.ds(j1, 8, stride=16), :]
         for c in range(3):
             k = side * 3 + c
             more = edges(k, xf3r, f3_low, f3_high)
-            more = more + p2[96 + k * 8 : 104 + k * 8, :] + ph[k * 8 : k * 8 + 8, :]
+            more = more + ph[k * 8 : k * 8 + 8, :]
             put_plane(vel, c, j, plane(vel, c, j) + c0 * more)
             more = edges(6 + k, xf3r, f3_low, f3_high)
             put_plane(vel, c, j1, plane(vel, c, j1) + c1 * more)
@@ -589,14 +601,14 @@
 
     scratch = [
         v(384, 128), v(384, 128), v(128, 128), v(n_gx, 16 * n_gx),
-        v(128, 128), v(384, 128), v(384, 128), v(384, 128), v(384, 128), v(192, 128),
+        v(128, 128), v(384, 128), v(384, 128), v(192, 128),
         v(n_gx, per, 256), v(n_gx, per, 256),
         v(3, 2, 3, 16, 128), v(2, 3, 16, 128), v(2, 3, 16, 128), v(2, 3, 16, 128),
     ]
     scratch += [v(2, 16, 128)] * 6
-    scratch += [v(96, 128), v(192, 128), v(192, 128)]
+    scratch += [v(96, 128), v(192, 128), v(48, 128), v(192, 128)]
     scratch += [v(2, 16, 128)] * 2 + [v(2, 8, 128)] * 2 + [v(2, 24, 128)] * 2 + [v(2, 8, 128)] * 2
-    scratch += [v(2, 6, 8, 128)] * 4 + [v(2, 3, 8, 128)] * 4
+    scratch += [v(2, 6, 8, 128)] * 2 + [v(2, 3, 8, 128)] * 6
     for n in (1, 3):
         scratch += [v(n * 32, 128)] * 3 + [v(2, n * 32, 128), v(2, 8, 128), v(2, 8, 128), v(2, 2, 8, 128)]
     scratch += [v(192, 128), v(288, 128), v(288, 128), v(288, 128), v(48, 128)]

time: 53.3 us -> 50.2 us (0.942)
  the two profiles are of different devices: /device:TPU:897 before, /device:TPU:657 now
where the time goes in v4:
time: 50.2 us; the launch traced here: 50 us
  Pallas kernels  49.4 us (98%)
  between operations  0.64 us (1%)
    pallas_call x1, Pallas kernels, on_device(): pl.pallas_call(functools.partial(kernel, sizes), out_shape=(jax.ShapeDtyp...  48.6 us

profile of v4, /device:TPU:657, one launch (start us, length us, event | category | flops | bytes accessed | tf_op | source)
XLA Modules:
  0.0 50.0 jit_solution(1329706900961318376)
XLA Ops:
  0.6 48.6 %vcycle.1 = (f32[384,128]{1,0:T(8,128)S(1)}, f32[3,16,4,128]{3,2,1,0:T(4,128)S(1)}) custom-call(f32[384,128]{1,0:T(8,128)} %bitcast.4, f32[384,128]{1,0:T(8,128)} %bitcast.5, f32[128,128]{1,0:T(8,128)} %bitcast.6, f32[32,512]{1,0:T(8,128)} %constant.2.clone.m_in), custom_call_target="tpu_custom_call" | custom-call | tf_op jit(solution)/shard_map/vcycle/pallas_call | solution.py:619
  49.3 0.7 %put.1 = (f32[384,128]{1,0:T(8,128)}, f32[3,16,4,128]{3,2,1,0:T(4,128)}) custom-call(f32[384,128]{1,0:T(8,128)S(1)} %get-tuple-element.6.velocity, f32[3,16,4,128]{3,2,1,0:T(4,128)S(1)} %get-tuple-element.7.compressed), custom_call_target="tpu_custom_call" | custom-call | tf_op jit(solution)/shard_map/put/pallas_call | solution.py:641

commit v5 on v4

--- a/solution.py
+++ b/solution.py
@@ -17,7 +17,7 @@
 MESH = pl.DeviceIdType.MESH
 F32 = jnp.float32
 
-X1, Z1, X2, Z2, X3, Z3, XF2, ZF2, XF3, ZF3, DZ, DX, DXZ, BZ, BX, BXZ, Y1, Y2, Y3, Y4, COUNT = range(21)
+X1, Z1, X2, Z2, X3, Z3, XF2, ZF2, XF3, ZF3, DZ, DX, DXZ, BZ, BX, BXZ, Y1, Y2, Y3, Y4, XC, COUNT = range(22)
 ROW = 4
 TURNS = (1, 1, 2, 2, 3, 3, 4, 5)
 
@@ -51,7 +51,7 @@
 def kernel(
     sizes, vp_in, f_in, r_in, m_in, vel, comp,
     vp, f, r, mcat, c_ref, u1, u2, tp, sendt, recvt,
-    xs, xr1, xr2, xr3, zs1, zr1, zs2, zr2, zs3, zr3,
+    xs, xr1, xr2, xr3, xcs, xcr, zs1, zr1, zs2, zr2, zs3, zr3,
     p1, p2, po, ps, xf2s, xf2r, zf2s, zf2r, xf3s, xf3r, zf3s, zf3r,
     y1s, y1r, y2s, y2r, y3s, y3r, y4s, y4r,
     down, dtile, dpack, dxr, dzs, dzr, dxz, bown, btile, bpack, bxr, bzs, bzr, bxz,
@@ -73,7 +73,7 @@
         return here[axis] > 0
 
     for ref in (
-        xr1, xr2, xr3, zr1, zr2, zr3, xf2r, zf2r, xf3r, zf3r, y1r, y2r, y3r, y4r, dzr, dxr, dxz, bzr, bxr, bxz
+        xr1, xr2, xr3, xcr, zr1, zr2, zr3, xf2r, zf2r, xf3r, zf3r, y1r, y2r, y3r, y4r, dzr, dxr, dxz, bzr, bxr, bxz
     ):
         ref[...] = jnp.zeros(ref.shape, F32)
 
@@ -86,9 +86,9 @@
 
     crossing_up = jnp.logical_and(place_x == ROW - 1, upper("gx"))
     crossing_down = jnp.logical_and(place_x == 0, lower("gx"))
-    last_pair = n_gy - 2
+    last_pair = n_gy - 1
     gy = here["gy"]
-    sure = ((gy == last_pair), jnp.logical_and(gy > 0, gy <= last_pair))
+    sure = (jnp.logical_and(gy == last_pair, upper("gy")), jnp.logical_and(gy > 0, gy <= last_pair))
     later = ((gy < last_pair), (gy > last_pair))
     greet(gy < last_pair, {"gy": gy + 1})
     greet(gy > last_pair, {"gy": gy - 1})
@@ -299,12 +299,12 @@
     mean_r = dot(tp[pl.ds(0, 32, stride=2), :] + tp[pl.ds(1, 32, stride=2), :], halves)
     inverse = damping / ((6.0 + 4.0 * mean_r) * 0.25)
     down[...] = inverse
-    stage_rows(down, y1s, 5, 1)
+    stage_rows(down, y2s, 3, 1)
     for slot, (j, k) in faces:
         for c in range(3):
             y1s[slot, c] = plane(vp, c, j)
         y1s[slot, 3] = c_ref[pl.ds(j, 8, stride=16), :]
-        y1s[slot, 4] = c_ref[pl.ds(k, 8, stride=16), :]
+        y3s[slot, 3] = c_ref[pl.ds(k, 8, stride=16), :]
     send_y(Y1, y1s, y1r, sure)
     fetches[2].wait()
     fetches[3].wait()
@@ -353,7 +353,14 @@
         )
         u2[c * 128 : (c + 1) * 128, :] = keep * u + c_ref[...] * total
     x_stage(u2, 2)
-    start(X3, "gx", both(xs.at[2]), xr3)
+    even, odd = pl.ds(0, 8, stride=2), pl.ds(1, 8, stride=2)
+    sums = [xs[2, side, c, even, :] + xs[2, side, c, odd, :] for side in (0, 1) for c in range(3)]
+    sums = dot(jnp.concatenate(sums, axis=0), halves)
+    for side in (0, 1):
+        first, second, third = (sums[(side * 3 + c) * 8 : (side * 3 + c + 1) * 8] for c in range(3))
+        xcs[side, 0] = jnp.where(lane8 < 64, first, pltpu.roll(second, 64, 1))
+        xcs[side, 1] = third
+    start(XC, "gx", both(xcs), xcr)
     z_stage(u2, zs3)
     start(Z3, "agg", both(zs3), zr3)
     for slot, (j, _) in faces:
@@ -371,30 +378,32 @@
             ends.append((message, "gy", both(src), dst, side))
     take_turn(2)
 
-    arrive(X3, "gx", both(xs.at[2]), xr3)
     arrive(Z3, "agg", both(zs3), zr3)
     z3_low, z3_high = zr3[0], zr3[1]
+    none = jnp.zeros((16, 128), F32)
     for c in range(3):
         u = comp_of(u2, c)
         res = (
             comp_of(f, c) - (6.0 + r[...]) * u
-            + around(u, xr3[0, c], xr3[1, c], spread(z3_low, c, 0), spread(z3_high, c, 127))
+            + around(u, none, none, spread(z3_low, c, 0), spread(z3_high, c, 127))
         )
         halved = res.reshape(4, 2, 16, 128)
         tp[c * 64 : (c + 1) * 64, :] = (
             (halved[:, 0] + halved[:, 1]).reshape(64, 128)
         )
     bown[...] = dot(tp[pl.ds(0, 96, stride=2), :] + tp[pl.ds(1, 96, stride=2), :], halves)
+    arrive(XC, "gx", both(xcs), xcr)
+    for side, i in ((0, 0), (1, 3)):
+        parts = (xcr[side, 0], pltpu.roll(xcr[side, 0], 64, 1), xcr[side, 1])
+        for c in range(3):
+            at = (c * 4 + i) * 8
+            bown[at : at + 8, :] = bown[at : at + 8, :] + parts[c]
     stage_rows(bown, y4s, 0, 3)
     start(Y4, "gy", both(y4s), y4r)
     take_turn(3)
 
 
     arrive(Y1, "gy", both(y1s), y1r)
-    unstage_rows(y1r, 5, dtile, 1)
-    join(down, dtile, dpack, dzs, 1)
-    start(DZ, "agg", both(dzs), dzr)
-    start(DX, "gx", (dpack, dpack), dxr)
     take_turn(4)
 
     for side, (j, _) in mine:
@@ -425,10 +434,11 @@
     arrive(XF2, "gx", both(xf2s), xf2r)
     arrive(ZF2, "agg", both(zf2s), zf2r)
     arrive(Y2, "gy", both(y2s), y2r)
+    arrive(Y3, "gy", both(y3s), y3r)
     f2_low, f2_high = zf2r[0], zf2r[1]
     for side, (j, j1) in mine:
         c0, c1 = c_ref[pl.ds(j, 8, stride=16), :], c_ref[pl.ds(j1, 8, stride=16), :]
-        ch0, ch1 = y1r[side, 3], y1r[side, 4]
+        ch0, ch1 = y1r[side, 3], y3r[side, 3]
         for c in range(3):
             k = side * 3 + c
             own, halo = p1[k * 8 : k * 8 + 8, :], p1[48 + k * 8 : 56 + k * 8, :]
@@ -447,11 +457,16 @@
     zf3s[1] = z_pack(tiles, 0, lane8)
     start(ZF3, "agg", both(zf3s), zf3r)
 
+    start(X3, "gx", both(xs.at[2]), xr3)
+
+    unstage_rows(y2r, 3, dtile, 1)
+    join(down, dtile, dpack, dzs, 1)
+    start(DZ, "agg", both(dzs), dzr)
+    start(DX, "gx", (dpack, dpack), dxr)
+
+    arrive(Y4, "gy", both(y4s), y4r)
     arrive(DZ, "agg", both(dzs), dzr)
     start(DXZ, "gx", (dzr, dzr), dxz)
-
-    arrive(Y3, "gy", both(y3s), y3r)
-    arrive(Y4, "gy", both(y4s), y4r)
     unstage_rows(y4r, 0, btile, 3)
     arrive(XF3, "gx", both(xf3s), xf3r)
     arrive(ZF3, "agg", both(zf3s), zf3r)
@@ -490,12 +505,11 @@
     start(BZ, "agg", both(bzs), bzr)
     start(BX, "gx", (bpack, bpack), bxr)
 
+    arrive(BZ, "agg", both(bzs), bzr)
+    start(BXZ, "gx", (bzr, bzr), bxz)
     arrive(DX, "gx", (dpack, dpack), dxr)
     arrive(DXZ, "gx", (dzr, dzr), dxz)
     cdext[...] = assemble(dpack, dzr, dxr, dxz, 0, 1)
-
-    arrive(BZ, "agg", both(bzs), bzr)
-    start(BXZ, "gx", (bzr, bzr), bxz)
 
     many = n_gx - 1
     lines = pltpu.make_async_remote_copy(
@@ -525,7 +539,6 @@
         jnp.logical_and(lane128 == 127, rows((128, 128)) == 64),
     )
     up = jnp.concatenate([jnp.where(fine, 1.0, 0.0), jnp.where(beyond, 1.0, 0.0)], axis=1).astype(F32)
-    none = jnp.zeros((16, 128), F32)
     for c in range(3):
         rhs_c = assemble(bpack, bzr, bxr, bxz, c, 3)
         weight = cdext[...]
@@ -549,6 +562,8 @@
                 spot = pl.ds(at + step, 4, stride=2)
                 ph[spot, :] = ph[spot, :] + line_
 
+    arrive(X3, "gx", both(xs.at[2]), xr3)
+
     def doubled(ref, c):
         value = ref[c * 96 + 16 : c * 96 + 80, :].reshape(4, 1, 16, 128)
         return jnp.broadcast_to(value, (4, 2, 16, 128)).reshape(128, 128)
@@ -604,11 +619,12 @@
         v(128, 128), v(384, 128), v(384, 128), v(192, 128),
         v(n_gx, per, 256), v(n_gx, per, 256),
         v(3, 2, 3, 16, 128), v(2, 3, 16, 128), v(2, 3, 16, 128), v(2, 3, 16, 128),
+        v(2, 2, 8, 128), v(2, 2, 8, 128),
     ]
     scratch += [v(2, 16, 128)] * 6
     scratch += [v(96, 128), v(192, 128), v(48, 128), v(192, 128)]
     scratch += [v(2, 16, 128)] * 2 + [v(2, 8, 128)] * 2 + [v(2, 24, 128)] * 2 + [v(2, 8, 128)] * 2
-    scratch += [v(2, 6, 8, 128)] * 2 + [v(2, 3, 8, 128)] * 6
+    scratch += [v(2, 4, 8, 128)] * 6 + [v(2, 3, 8, 128)] * 2
     for n in (1, 3):
         scratch += [v(n * 32, 128)] * 3 + [v(2, n * 32, 128), v(2, 8, 128), v(2, 8, 128), v(2, 2, 8, 128)]
     scratch += [v(192, 128), v(288, 128), v(288, 128), v(288, 128), v(48, 128)]

time: 50.2 us -> 47.1 us (0.938)
  the two profiles are of different devices: /device:TPU:657 before, /device:TPU:263 now
where the time goes in v5:
time: 47.1 us; the launch traced here: 46.9 us
  Pallas kernels  46.3 us (98%)
  between operations  0.64 us (1%)
    pallas_call x1, Pallas kernels, on_device(): pl.pallas_call(functools.partial(kernel, sizes), out_shape=(jax.ShapeDtyp...  45.6 us

profile of v5, /device:TPU:263, one launch (start us, length us, event | category | flops | bytes accessed | tf_op | source)
XLA Modules:
  0.0 46.9 jit_solution(573175468302529914)
XLA Ops:
  0.6 45.6 %vcycle.1 = (f32[384,128]{1,0:T(8,128)S(1)}, f32[3,16,4,128]{3,2,1,0:T(4,128)S(1)}) custom-call(f32[384,128]{1,0:T(8,128)} %bitcast.4, f32[384,128]{1,0:T(8,128)} %bitcast.5, f32[128,128]{1,0:T(8,128)} %bitcast.6, f32[32,512]{1,0:T(8,128)} %constant.2.clone.m_in), custom_call_target="tpu_custom_call" | custom-call | tf_op jit(solution)/shard_map/vcycle/pallas_call | solution.py:635
  46.2 0.7 %put.1 = (f32[384,128]{1,0:T(8,128)}, f32[3,16,4,128]{3,2,1,0:T(4,128)}) custom-call(f32[384,128]{1,0:T(8,128)S(1)} %get-tuple-element.6.velocity, f32[3,16,4,128]{3,2,1,0:T(4,128)S(1)} %get-tuple-element.7.compressed), custom_call_target="tpu_custom_call" | custom-call | tf_op jit(solution)/shard_map/put/pallas_call | solution.py:657

commit v6 on v5

--- a/solution.py
+++ b/solution.py
@@ -17,7 +17,7 @@
 MESH = pl.DeviceIdType.MESH
 F32 = jnp.float32
 
-X1, Z1, X2, Z2, X3, Z3, XF2, ZF2, XF3, ZF3, DZ, DX, DXZ, BZ, BX, BXZ, Y1, Y2, Y3, Y4, XC, COUNT = range(22)
+X1, Z1, X2, Z2, X3, Z3, XF2, ZF2, XF3, ZF3, DZ, DX, BZ, BX, Y1, Y2, Y3, Y4, XC, COUNT = range(20)
 ROW = 4
 TURNS = (1, 1, 2, 2, 3, 3, 4, 5)
 
@@ -56,7 +56,7 @@
     y1s, y1r, y2s, y2r, y3s, y3r, y4s, y4r,
     down, dtile, dpack, dxr, dzs, dzr, dxz, bown, btile, bpack, bxr, bzs, bzr, bxz,
     cdext, cf, cz, eu, ph,
-    insem, ssem, rsem, assem, arsem, ready, token_up, token_down,
+    insem, ssem, rsem, cssem, crsem, assem, arsem, ready, token_up, token_down,
 ):
     n_agg, n_gx, n_gy = sizes
     per = 128 // n_gx
@@ -100,6 +100,19 @@
         )
     greet(crossing_up, {"gx": gx + 1})
     greet(crossing_down, {"gx": gx - 1})
+    corners = [
+        (x_side, z_side, sx, sz)
+        for x_side, sx in ((0, 1), (1, -1))
+        for z_side, sz in ((0, 1), (1, -1))
+    ]
+
+    def corner_there(sx, sz):
+        return jnp.logical_and(
+            upper("gx") if sx == 1 else lower("gx"), upper("agg") if sz == 1 else lower("agg")
+        )
+
+    for _, _, sx, sz in corners:
+        greet(corner_there(sx, sz), {"gx": gx + sx, "agg": here["agg"] + sz})
     greet(level < levels - 1, {"gx": gx + ROW})
     greet(level > 0, {"gx": gx - ROW})
 
@@ -142,6 +155,29 @@
             @pl.when(lower(axis) if side == 0 else upper(axis))
             def _(side=side):
                 one_copy(message, axis, src, dst, side).wait_recv()
+
+    def corner_copy(kind, x_side, z_side, sx, sz):
+        src, dst = ((dzs, dxz), (bzs, bxz))[kind]
+        k = x_side * 2 + z_side
+        return pltpu.make_async_remote_copy(
+            src_ref=src.at[z_side], dst_ref=dst.at[x_side, z_side],
+            send_sem=cssem.at[kind, k], recv_sem=crsem.at[kind, k],
+            device_id={"gx": gx + sx, "agg": here["agg"] + sz}, device_id_type=MESH,
+        )
+
+    def start_corners(kind):
+        for corner in corners:
+
+            @pl.when(corner_there(*corner[2:]))
+            def _(corner=corner):
+                corner_copy(kind, *corner).start()
+
+    def arrive_corners(kind):
+        for corner in corners:
+
+            @pl.when(corner_there(-corner[2], -corner[3]))
+            def _(corner=corner):
+                corner_copy(kind, *corner).wait_recv()
 
     def both(ref):
         return (ref.at[0], ref.at[1])
@@ -279,6 +315,8 @@
         sure[0], sure[1], upper("agg"), lower("agg"), crossing_up, crossing_down, level < levels - 1, level > 0
     ):
         greeted = greeted + test.astype(jnp.int32)
+    for _, _, sx, sz in corners:
+        greeted = greeted + corner_there(sx, sz).astype(jnp.int32)
     pl.semaphore_wait(barrier, greeted)
 
     for test, step in zip(sure, (1, -1)):
@@ -418,6 +456,8 @@
     zf2s[0] = z_pack(tiles, 127, lane8)
     zf2s[1] = z_pack(tiles, 0, lane8)
     start(ZF2, "agg", both(zf2s), zf2r)
+
+    start(X3, "gx", both(xs.at[2]), xr3)
 
     take_turn(5)
 
@@ -457,16 +497,13 @@
     zf3s[1] = z_pack(tiles, 0, lane8)
     start(ZF3, "agg", both(zf3s), zf3r)
 
-    start(X3, "gx", both(xs.at[2]), xr3)
-
     unstage_rows(y2r, 3, dtile, 1)
     join(down, dtile, dpack, dzs, 1)
     start(DZ, "agg", both(dzs), dzr)
+    start_corners(0)
     start(DX, "gx", (dpack, dpack), dxr)
 
     arrive(Y4, "gy", both(y4s), y4r)
-    arrive(DZ, "agg", both(dzs), dzr)
-    start(DXZ, "gx", (dzr, dzr), dxz)
     unstage_rows(y4r, 0, btile, 3)
     arrive(XF3, "gx", both(xf3s), xf3r)
     arrive(ZF3, "agg", both(zf3s), zf3r)
@@ -503,13 +540,9 @@
                     ref[at, :] = ref[at, :] + line[base + part : base + part + 4]
     join(bown, btile, bpack, bzs, 3)
     start(BZ, "agg", both(bzs), bzr)
+    start_corners(1)
     start(BX, "gx", (bpack, bpack), bxr)
 
-    arrive(BZ, "agg", both(bzs), bzr)
-    start(BXZ, "gx", (bzr, bzr), bxz)
-    arrive(DX, "gx", (dpack, dpack), dxr)
-    arrive(DXZ, "gx", (dzr, dzr), dxz)
-    cdext[...] = assemble(dpack, dzr, dxr, dxz, 0, 1)
 
     many = n_gx - 1
     lines = pltpu.make_async_remote_copy(
@@ -529,8 +562,13 @@
                 value = value + wide[at : at + 16, m * 4 * n_gx : (m + 1) * 4 * n_gx]
             comp[c, :, k, :] = value
 
+    arrive(DZ, "agg", both(dzs), dzr)
+    arrive(DX, "gx", (dpack, dpack), dxr)
+    arrive_corners(0)
+    cdext[...] = assemble(dpack, dzr, dxr, dxz, 0, 1)
+    arrive(BZ, "agg", both(bzs), bzr)
     arrive(BX, "gx", (bpack, bpack), bxr)
-    arrive(BXZ, "gx", (bzr, bzr), bxz)
+    arrive_corners(1)
 
     y16 = lax.rem(rows((192, 128)), 16)
     fine = lane128 // 2 == rows((128, 128))
@@ -595,6 +633,13 @@
         def _(args=(message, axis, src, dst, side)):
             one_copy(*args).wait_send()
 
+    for corner in corners:
+
+        @pl.when(corner_there(*corner[2:]))
+        def _(corner=corner):
+            for kind in (0, 1):
+                corner_copy(kind, *corner).wait_send()
+
 
 def put_kernel(velocity, compressed, velocity_out, compressed_out, sem):
     copies = [
@@ -629,7 +674,7 @@
         scratch += [v(n * 32, 128)] * 3 + [v(2, n * 32, 128), v(2, 8, 128), v(2, 8, 128), v(2, 2, 8, 128)]
     scratch += [v(192, 128), v(288, 128), v(288, 128), v(288, 128), v(48, 128)]
     dma = pltpu.SemaphoreType.DMA
-    scratch += [dma((4,)), dma((COUNT, 2)), dma((COUNT, 2)), dma, dma]
+    scratch += [dma((4,)), dma((COUNT, 2)), dma((COUNT, 2)), dma((2, 4)), dma((2, 4)), dma, dma]
     scratch += [pltpu.SemaphoreType.REGULAR] * 3
     vmem = pl.BlockSpec(memory_space=pltpu.VMEM)
     velocity, compressed = pl.pallas_call(

time: 47.1 us -> 46.3 us (0.983)
  the two profiles are of different devices: /device:TPU:263 before, /device:TPU:103 now
where the time goes in v6:
time: 46.3 us; the launch traced here: 46.1 us
  Pallas kernels  45.5 us (98%)
  between operations  0.64 us (1%)
    pallas_call x1, Pallas kernels, on_device(): pl.pallas_call(functools.partial(kernel, sizes), out_shape=(jax.ShapeDtyp...  44.7 us

profile of v6, /device:TPU:103, one launch (start us, length us, event | category | flops | bytes accessed | tf_op | source)
XLA Modules:
  0.0 46.1 jit_solution(1853305719956958552)
XLA Ops:
  0.6 44.7 %vcycle.1 = (f32[384,128]{1,0:T(8,128)S(1)}, f32[3,16,4,128]{3,2,1,0:T(4,128)S(1)}) custom-call(f32[384,128]{1,0:T(8,128)} %bitcast.4, f32[384,128]{1,0:T(8,128)} %bitcast.5, f32[128,128]{1,0:T(8,128)} %bitcast.6, f32[32,512]{1,0:T(8,128)} %constant.2.clone.m_in), custom_call_target="tpu_custom_call" | custom-call | tf_op jit(solution)/shard_map/vcycle/pallas_call | solution.py:680
  45.4 0.7 %put.1 = (f32[384,128]{1,0:T(8,128)}, f32[3,16,4,128]{3,2,1,0:T(4,128)}) custom-call(f32[384,128]{1,0:T(8,128)S(1)} %get-tuple-element.6.velocity, f32[3,16,4,128]{3,2,1,0:T(4,128)S(1)} %get-tuple-element.7.compressed), custom_call_target="tpu_custom_call" | custom-call | tf_op jit(solution)/shard_map/put/pallas_call | solution.py:702
